TPU v7x, 128 devices: a whole 4x4x4 slice. The times are simulated.
128 devices in a mesh: att: 2 (over core), emb: 64 (over z, y, x).
Axes of the slice: x: 4, y: 4, z: 4, core: 2. Of those that a mesh axis runs over, the one named last changes fastest.
Arguments:
- w_qkv: float32 [4, 3, 1024, 1024], P(None, None, 'emb', 'att')
- w_out: float32 [4, 1024, 1024], P(None, 'att', 'emb')
- x_in: bfloat16 [4, 8192, 1024], P(None, None, 'emb')
- dy_qkv: bfloat16 [4, 3, 8192, 1024], P(None, None, None, 'att')
- x_attn: bfloat16 [4, 8192, 1024], P(None, None, 'att')
- dy_out: bfloat16 [4, 8192, 1024], P(None, None, 'emb')
- r_qkv: float32 [4, 3, 1024], P(None, None, 'emb')
- c_qkv: float32 [4, 3, 1024], P(None, None, 'att')
- r_out: float32 [4, 1024], P(None, 'att')
- c_out: float32 [4, 1024], P(None, 'emb')
- hyper_params: float32 [3], replicated
Outputs:
- output 1: float32 [4, 3, 1024, 1024], P(None, None, 'emb', 'att')
- output 2: float32 [4, 1024, 1024], P(None, 'att', 'emb')
- output 3: float32 [4, 3, 1024], P(None, None, 'emb')
- output 4: float32 [4, 3, 1024], P(None, None, 'att')
- output 5: float32 [4, 1024], P(None, 'att')
- output 6: float32 [4, 1024], P(None, 'emb')
All inputs are finite; a program needn't handle non-finite values.
Results may differ from a plain program's by a relative error of at most 0.001.
Values are sent between devices in bfloat16 or wider.
A program may use at most 1 GiB of HBM per device.

v0:
```python
import jax
import jax.numpy as jnp
from jax import lax
from jax.sharding import PartitionSpec as P

EPS_SQUARE = 1e-30
EPS_SCALE = 1e-3


def factored_step(w_grad, weight, row_old, col_old, hyper_params, m_axis, n_axis, m_total, n_total):
    beta_two = hyper_params[0]
    rel_step = hyper_params[1]
    clip_limit = hyper_params[2]
    q_sq = w_grad * w_grad + EPS_SQUARE
    row_part = jnp.sum(q_sq, axis=2)
    col_part = jnp.sum(q_sq, axis=1)
    lead_flag = (lax.axis_index(n_axis) == 0).astype(jnp.float32)
    scalar_part = jnp.stack(
        [jnp.sum(col_part, axis=1), jnp.sum(weight * weight, axis=(1, 2)), lead_flag * jnp.sum(row_old, axis=1)],
        axis=1,
    )
    row_sum = lax.psum(row_part, n_axis)
    col_sum = lax.psum(col_part, m_axis)
    scalar_sum = lax.psum(scalar_part, (m_axis, n_axis))
    n_elems = m_total * n_total
    row_new = beta_two * row_old + (1.0 - beta_two) * (row_sum / n_total)
    col_new = beta_two * col_old + (1.0 - beta_two) * (col_sum / m_total)
    mean_row = beta_two * scalar_sum[:, 2] / m_total + (1.0 - beta_two) * scalar_sum[:, 0] / n_elems
    row_factor = lax.rsqrt(row_new / mean_row[:, None])
    col_factor = lax.rsqrt(col_new)
    update = w_grad * row_factor[:, :, None] * col_factor[:, None, :]
    u_sum = lax.psum(jnp.sum(update * update, axis=(1, 2)), (m_axis, n_axis))
    rms_u = jnp.sqrt(u_sum / n_elems)
    rms_w = jnp.sqrt(scalar_sum[:, 1] / n_elems)
    step_size = rel_step * jnp.maximum(EPS_SCALE, rms_w) / jnp.maximum(1.0, rms_u / clip_limit)
    return weight - step_size[:, None, None] * update, row_new, col_new


def solution(mesh):
    emb_size = mesh.shape["emb"]
    att_size = mesh.shape["att"]
    in_specs = (
        P(None, None, "emb", "att"),
        P(None, "att", "emb"),
        P(None, None, "emb"),
        P(None, None, None, "att"),
        P(None, None, "att"),
        P(None, None, "emb"),
        P(None, None, "emb"),
        P(None, None, "att"),
        P(None, "att"),
        P(None, "emb"),
        P(),
    )
    out_specs = (
        P(None, None, "emb", "att"),
        P(None, "att", "emb"),
        P(None, None, "emb"),
        P(None, None, "att"),
        P(None, "att"),
        P(None, "emb"),
    )

    def local_run(w_qkv, w_out, x_in, dy_qkv, x_attn, dy_out, r_qkv, c_qkv, r_out, c_out, hyper_params):
        d_model = x_in.shape[2] * emb_size
        inner_dim = x_attn.shape[2] * att_size
        per_layer = []
        for layer_idx in range(w_qkv.shape[0]):
            g_qkv = jnp.einsum("td,ktn->kdn", x_in[layer_idx], dy_qkv[layer_idx], preferred_element_type=jnp.float32)
            new_qkv = factored_step(
                g_qkv, w_qkv[layer_idx], r_qkv[layer_idx], c_qkv[layer_idx], hyper_params, "emb", "att", d_model, inner_dim
            )
            g_out = jnp.einsum("ti,td->id", x_attn[layer_idx], dy_out[layer_idx], preferred_element_type=jnp.float32)
            new_out = factored_step(
                g_out[None], w_out[layer_idx][None], r_out[layer_idx][None], c_out[layer_idx][None],
                hyper_params, "att", "emb", inner_dim, d_model
            )
            per_layer.append((new_qkv[0], new_out[0][0], new_qkv[1], new_qkv[2], new_out[1][0], new_out[2][0]))
        return tuple(jnp.stack([layer_out[out_slot] for layer_out in per_layer]) for out_slot in range(6))

    return jax.shard_map(local_run, mesh=mesh, in_specs=in_specs, out_specs=out_specs, check_vma=False)
```

profile of v0, /device:TPU:1, one launch (start us, length us, event | category | flops | bytes accessed | tf_op | source)
XLA Modules:
  0.0 720.9 jit_solution(16267149028958147797)
XLA Ops:
  0.7 1.4 fusion.97
  2.7 1.5 slice_reduce_fusion.3
  7.8 1.5 multiply_reduce_fusion.11
  9.3 1.6 slice_multiply_fusion.3
  11.9 5.3 fusion.64
  18.4 5.3 fusion.61
  23.7 1.4 pad_maximum_fusion.10
  25.1 5.3 fusion.70
  30.4 1.4 pad_maximum_fusion.13
  31.7 5.3 fusion.67
  37.0 1.4 pad_maximum_fusion.12
  38.4 68.6 %all-reduce.1 = (f32[1,3]{1,0:T(1,128)S(1)}, f32[1,3]{1,0:T(1,128)S(1)}, f32[1,3]{1,0:T(1,128)S(1)}, f32[1,3]{1,0:T(1,128)S(1)}) all-reduce(f32[1,3]{1,0:T(1,128)S(1)} %pad_maximum_fusion.13, f32[1,3]{1,0:T(1,128)S(1)} %pad_maximum_fusion.12, f32[1,3]{1,0:T(1,128)S(1)} %pad_maximum_fusion.11, ...), channel_id=1, replica_groups=mesh['att'=2,'emb'=64] {'att','emb'}, use_global_device_ids=true, to_apply=%region_73.0 | all-reduce | flops 12 | bytes 96 | tf_op jit(solution)/shard_map/psum | solution.py:24
  121.3 10.0 %fusion.52 = (f32[3,16]{1,0:T(4,128)S(1)}, f32[3,512]{1,0:T(4,128)S(1)}, f32[3]{0:T(128)S(1)}, f32[3,512,16]{1,2,0:T(8,128)S(1)}) fusion(bf16[4,3,8192,512]{3,2,1,0:T(8,128)(2,1)} %param.14, bf16[4,8192,16]{1,2,0:T(8,128)(2,1)S(1)} %copy-done.4), kind=kOutput, calls=%fused_computation.74 | convolution fusion | flops 402774464 | bytes 25532620 | tf_op jit(solution)/shard_map/td,ktn->kdn/dot_general | solution.py:69
  131.4 10.1 %fusion.49 = (f32[3,16]{1,0:T(4,128)S(1)}, f32[3,512]{1,0:T(4,128)S(1)}, f32[3]{0:T(128)S(1)}, f32[3,512,16]{1,2,0:T(8,128)S(1)}) fusion(bf16[4,3,8192,512]{3,2,1,0:T(8,128)(2,1)} %param.14, bf16[4,8192,16]{1,2,0:T(8,128)(2,1)S(1)} %copy-done.4), kind=kOutput, calls=%fused_computation.71 | convolution fusion | flops 402774464 | bytes 25532620 | tf_op jit(solution)/shard_map/td,ktn->kdn/dot_general | solution.py:69
  141.4 10.0 %fusion.58 = (f32[3,16]{1,0:T(4,128)S(1)}, f32[3,512]{1,0:T(4,128)S(1)}, f32[3]{0:T(128)S(1)}, f32[3,512,16]{1,2,0:T(8,128)S(1)}) fusion(bf16[4,3,8192,512]{3,2,1,0:T(8,128)(2,1)} %param.14, bf16[4,8192,16]{1,2,0:T(8,128)(2,1)S(1)} %copy-done.4), kind=kOutput, calls=%fused_computation.80 | convolution fusion | flops 402774464 | bytes 25532620 | tf_op jit(solution)/shard_map/td,ktn->kdn/dot_general | solution.py:69
  151.5 10.0 %fusion.55 = (f32[3,16]{1,0:T(4,128)S(1)}, f32[3,512]{1,0:T(4,128)S(1)}, f32[3]{0:T(128)S(1)}, f32[3,512,16]{1,2,0:T(8,128)S(1)}) fusion(bf16[4,3,8192,512]{3,2,1,0:T(8,128)(2,1)} %param.14, bf16[4,8192,16]{1,2,0:T(8,128)(2,1)S(1)} %copy-done.4), kind=kOutput, calls=%fused_computation.77 | convolution fusion | flops 402774464 | bytes 25532620 | tf_op jit(solution)/shard_map/td,ktn->kdn/dot_general | solution.py:69
  161.5 4.1 all-reduce.5
  165.6 62.1 %all-reduce.3 = (f32[3,3]{0,1:T(4,128)S(1)}, f32[3,3]{0,1:T(4,128)S(1)}, f32[3,3]{0,1:T(4,128)S(1)}, f32[3,3]{0,1:T(4,128)S(1)}) all-reduce(f32[3,3]{0,1:T(4,128)S(1)} %pad_maximum_fusion.8, f32[3,3]{0,1:T(4,128)S(1)} %pad_maximum_fusion.7, f32[3,3]{0,1:T(4,128)S(1)} %pad_maximum_fusion.6, ...), channel_id=1, replica_groups=mesh['att'=2,'emb'=64] {'emb','att'}, use_global_device_ids=true, to_apply=%region_33.0 | all-reduce | flops 36 | bytes 288 | tf_op jit(solution)/shard_map/psum | solution.py:24
  231.2 290.2 %all-reduce.4 = (f32[3,512]{1,0:T(4,128)S(1)}, f32[3,512]{1,0:T(4,128)S(1)}, f32[3,512]{1,0:T(4,128)S(1)}, f32[3,512]{1,0:T(4,128)S(1)}, f32[1,512]{1,0:T(1,128)...) all-reduce(f32[3,512]{1,0:T(4,128)S(1)} %get-tuple-element.36, ...), channel_id=1, replica_groups=mesh['att'=2,'emb'=64] {'emb'}, use_global_device_ids=true, to_apply=%region_37.0 | all-reduce | flops 8192 | bytes 65536 | tf_op jit(solution)/shard_map/psum | solution.py:23
  526.6 116.8 %all-reduce = (f32[1]{0:T(128)}, f32[1]{0:T(128)}, f32[1]{0:T(128)}, f32[1]{0:T(128)}) all-reduce(f32[1]{0:T(128)} %bitcast.113, f32[1]{0:T(128)} %bitcast.97, f32[1]{0:T(128)} %bitcast.81, f32[1]{0:T(128)} %bitcast.65), channel_id=1, replica_groups=mesh['att'=2,'emb'=64] {'att','emb'}, use_global_device_ids=true, to_apply=%region_79.0 | all-reduce | flops 4 | bytes 32 | tf_op jit(solution)/shard_map/psum | solution.py:32
  651.5 62.5 %all-reduce.2 = (f32[3]{0:T(128)S(1)}, f32[3]{0:T(128)S(1)}, f32[3]{0:T(128)S(1)}, f32[3]{0:T(128)S(1)}) all-reduce(f32[3]{0:T(128)S(1)} %multiply_reduce_fusion, f32[3]{0:T(128)S(1)} %multiply_reduce_fusion.1, f32[3]{0:T(128)S(1)} %multiply_reduce_fusion.2, ...), channel_id=1, replica_groups=mesh['att'=2,'emb'=64] {'emb','att'}, use_global_device_ids=true, to_apply=%region_39.0 | all-reduce | flops 12 | bytes 96 | tf_op jit(solution)/shard_map/psum | solution.py:32
  715.3 1.3 bitcast_divide_fusion.2
  716.6 1.3 bitcast_divide_fusion.1
  718.1 1.3 bitcast_divide_fusion
  (55 shorter events, 18.8 us)
Async XLA Ops:
  0.6 120.7 %copy-start.4 = (bf16[4,8192,16]{1,2,0:T(8,128)(2,1)S(1)}, bf16[4,8192,16]{1,2,0:T(8,128)(2,1)}, u32[]{:S(2)}) copy-start(bf16[4,8192,16]{1,2,0:T(8,128)(2,1)} %param.13) | copy-start | bytes 3145732
  131.3 98.6 %copy-start.3 = (f32[4,16]{1,0:T(4,128)S(1)}, f32[4,16]{1,0:T(4,128)}, u32[]{:S(2)}) copy-start(f32[4,16]{1,0:T(4,128)} %param.20) | copy-start | bytes 772
  131.3 391.8 %copy-start.2 = (f32[4,512]{1,0:T(4,128)S(1)}, f32[4,512]{1,0:T(4,128)}, u32[]{:S(2)}) copy-start(f32[4,512]{1,0:T(4,128)} %param.19) | copy-start | bytes 24580
  131.3 517.7 %copy-start.1 = (f32[4,512,16]{1,2,0:T(8,128)S(1)}, f32[4,512,16]{1,2,0:T(8,128)}, u32[]{:S(2)}) copy-start(f32[4,512,16]{1,2,0:T(8,128)} %param.12) | copy-start | bytes 393220
  131.4 586.6 %copy-start = (f32[4,3,16,512]{3,2,1,0:T(8,128)S(1)}, f32[4,3,16,512]{3,2,1,0:T(8,128)}, u32[]{:S(2)}) copy-start(f32[4,3,16,512]{3,2,1,0:T(8,128)} %param.11) | copy-start | bytes 1179652
where the time goes:
time: 722 us; the launch traced here: 721 us
  blocking collectives  604 us (84%)
  matrix products  61.2 us (8%)
  other arithmetic  27.9 us (4%)
  between operations  22.6 us (3%)
    psum x1, blocking collectives, factored_step(): col_sum = lax.psum(col_part, m_axis)  290 us
    psum x2, blocking collectives, factored_step(): u_sum = lax.psum(jnp.sum(update * update, axis=(1, 2)), (m_axis, n_axis))  179 us
    psum x2, blocking collectives, factored_step(): scalar_sum = lax.psum(scalar_part, (m_axis, n_axis))  131 us
    dot_general x4, matrix products, local_run(): jnp.einsum('td,ktn->kdn', x_in[layer_idx], dy_qkv[layer_idx], preferred_e...  40.1 us
    dot_general x4, matrix products, local_run(): jnp.einsum('ti,td->id', x_attn[layer_idx], dy_out[layer_idx], preferred_e...  21.1 us

commit v1 on v0

v1 whole, which is shorter than its diff:
```python
import functools

import jax
import jax.numpy as jnp
from jax import lax
from jax.experimental import pallas as pl
from jax.experimental.pallas import tpu as pltpu
from jax.sharding import PartitionSpec as P

EPS_SQUARE = 1e-30
EPS_SCALE = 1e-3
T_SCALE = 2.0**32

RING = 4
X, Y, Z = 0, 1, 2
STRIDES = (1, 4, 16)

UNITS = (
    (0, 0, X),
    (0, 1, Y),
    (1, 0, Y),
    (1, 1, Z),
    (2, 0, Z),
    (3, 0, X),
    (2, 1, None),
    (3, 1, None),
)
BATCHES = (
    ((0, 0), (0, 1), (0, 2), (0, 3)),
    ((1, 0), (1, 1), (1, 2), (1, 3)),
    ((2, 0), (2, 1), (2, 2)),
    ((3, 0), (3, 1), (3, 2), (2, 3)),
    ((3, 3),),
)
PLAN = (
    ("U", 0), ("U", 1), ("U", 2), ("R", 0), ("U", 3), ("D", 0), ("U", 4), ("R", 1), ("S1", 0), ("U", 5), ("D", 1),
    ("R", 2), ("S2", 0), ("S1", 1), ("D", 2), ("U", 6), ("R", 3), ("F", 0), ("S2", 1), ("S1", 2), ("D", 3),
    ("U", 7), ("R", 4), ("W", 0), ("F", 1), ("S2", 2), ("S1", 3), ("D", 4),
    ("W", 1), ("F", 2), ("S2", 3), ("S1", 4), ("W", 2), ("F", 3), ("S2", 4), ("W", 3), ("F", 4), ("W", 4),
)

GROUPED = tuple(u for u, unit in enumerate(UNITS) if unit[2] is not None)
WHOLE = tuple(u for u, unit in enumerate(UNITS) if unit[2] is None)


def mats_of(unit):
    layer, kind, _ = unit
    return tuple((layer, m) for m in range(3)) if kind == 0 else ((layer, 3),)


GROUPED_MATS = tuple(mat for u in GROUPED for mat in mats_of(UNITS[u]))
AXIS_OF = {mat: UNITS[u][2] for u in GROUPED for mat in mats_of(UNITS[u])}


def kernel(
    tokens, width, att_size,
    w_qkv, w_out, x_in, dy_qkv, x_attn, dy_out, r_qkv, c_qkv, r_out, c_out, hyper,
    w_qkv_new, w_out_new, r_qkv_new, c_qkv_new, r_out_new, c_out_new,
    dy_part, dy_whole, x_part, x_whole, g_part, g_got, g_all, wq, wo, rq, cq, ro, co,
    pair_out, pair_in, stage, fin_out, fin_in,
    small_sem, own_sem, dy_sem, x_send, x_recv, g_send, g_recv, pair_send, pair_recv, st_send, st_recv, fin_send, fin_recv,
    out_sem,
):
    beta_two, rel_step, clip_limit = hyper[0], hyper[1], hyper[2]
    att = lax.axis_index("att")
    emb = lax.axis_index("emb")
    coords = tuple(lax.rem(emb // stride, RING) for stride in STRIDES)
    part = tokens // RING
    n_elems = float(width * width)

    def peer(axis, k):
        place = lax.rem(coords[axis] + k, RING)
        return (att, emb + (place - coords[axis]) * STRIDES[axis]), place

    partner = (lax.rem(att + 1, att_size), emb)

    def remote(src, dst, send, recv, device):
        return pltpu.make_async_remote_copy(
            src_ref=src, dst_ref=dst, send_sem=send, recv_sem=recv, device_id=device, device_id_type=pl.DeviceIdType.MESH
        )

    small = [
        pltpu.make_async_copy(src, dst, small_sem.at[i])
        for i, (src, dst) in enumerate(
            ((w_qkv, wq), (w_out, wo), (r_qkv, rq), (c_qkv, cq), (r_out, ro), (c_out, co))
        )
    ]
    for copy in small:
        copy.start()

    def x_source(u):
        layer, kind, _ = UNITS[u]
        return (x_in, dy_out)[kind].at[layer]

    def x_own(u):
        if u in GROUPED:
            here = coords[UNITS[u][2]]
            src = x_source(u).at[:, pl.ds(pl.multiple_of(here * part, part), part)]
            return pltpu.make_async_copy(src, x_part.at[GROUPED.index(u), here], own_sem.at[u])
        return pltpu.make_async_copy(x_source(u), x_whole.at[WHOLE.index(u)], own_sem.at[u])

    def x_copy(u, k):
        axis = UNITS[u][2]
        device, there = peer(axis, k)
        slot = GROUPED.index(u)
        src = x_source(u).at[:, pl.ds(pl.multiple_of(there * part, part), part)]
        return remote(src, x_part.at[slot, coords[axis]], x_send.at[slot, k - 1], x_recv.at[slot, k - 1], device)

    def dy_source(mat):
        layer, m = mat
        return dy_qkv.at[layer, m] if m < 3 else x_attn.at[layer]

    def dy_copies(u):
        out = []
        for mat in mats_of(UNITS[u]):
            if u in GROUPED:
                i = GROUPED_MATS.index(mat)
                here = coords[UNITS[u][2]]
                src = dy_source(mat).at[pl.ds(pl.multiple_of(here * part, part), part), :]
                out.append(pltpu.make_async_copy(src, dy_part.at[i], dy_sem.at[i]))
            else:
                for j in range(RING):
                    w = WHOLE.index(u)
                    rows = pl.ds(j * part, part)
                    out.append(
                        pltpu.make_async_copy(
                            dy_source(mat).at[rows, :], dy_whole.at[w, rows, :], dy_sem.at[len(GROUPED_MATS) + w * RING + j]
                        )
                    )
        return out

    for u in range(len(UNITS)):
        x_own(u).start()
        for copy in dy_copies(u):
            copy.start()

    barrier = pltpu.get_barrier_semaphore()
    neighbours = [peer(axis, k)[0] for axis in (X, Y, Z) for k in range(1, RING)] + [partner]
    for device in neighbours:
        pl.semaphore_signal(barrier, inc=1, device_id=device, device_id_type=pl.DeviceIdType.MESH)
    pl.semaphore_wait(barrier, len(neighbours))

    for u in GROUPED:
        for k in (1, 3, 2):
            x_copy(u, k).start()

    def g_copy(mat, k):
        axis = AXIS_OF[mat]
        device, there = peer(axis, k)
        i = GROUPED_MATS.index(mat)
        return remote(g_part.at[i, there], g_got.at[i, k - 1], g_send.at[i, k - 1], g_recv.at[i, k - 1], device)

    def slot_of(mat):
        return mat[0] * 4 + mat[1]

    def products(u):
        x_own(u).wait()
        copies = dy_copies(u)
        if u in GROUPED:
            for k in range(1, RING):
                x_copy(u, k).wait_recv()
            lhs = x_part.at[GROUPED.index(u)]
            for mat, copy in zip(mats_of(UNITS[u]), copies):
                i = GROUPED_MATS.index(mat)
                copy.wait()
                got = jnp.dot(
                    lhs[...].reshape(RING * 16, part), dy_part[i], preferred_element_type=jnp.float32
                )
                g_part[i] = got.reshape(RING, 16, got.shape[1])
                for k in range(1, RING):
                    g_copy(mat, k).start()
        else:
            w = WHOLE.index(u)
            (mat,) = mats_of(UNITS[u])
            total = None
            for j, copy in enumerate(copies):
                copy.wait()
                rows = pl.ds(j * part, part)
                got = jnp.dot(x_whole[w, :, rows], dy_whole[w, rows, :], preferred_element_type=jnp.float32)
                total = got if total is None else total + got
            g_all[slot_of(mat)] = total

    diag = lax.broadcasted_iota(jnp.int32, (16, 16), 0) == lax.broadcasted_iota(jnp.int32, (16, 16), 1)
    lane = lax.broadcasted_iota(jnp.int32, (16, 128), 1)

    def up(row):
        return jnp.sum(jnp.where(diag, jnp.broadcast_to(row, (16, 16)), 0.0), axis=1, keepdims=True)

    def across(column):
        return jnp.sum(jnp.where(diag, jnp.broadcast_to(column, (16, 16)), 0.0), axis=0, keepdims=True)

    def pair_copy(b):
        return remote(pair_out.at[b], pair_in.at[b], pair_send.at[b], pair_recv.at[b], partner)

    def stage_copies(b, s):
        here = coords[s]
        out = []
        for k in range(1, RING):
            device, _ = peer(s, k)
            slot = stage.at[b, s, here]
            out.append(remote(slot, slot, st_send.at[b, s, k - 1], st_recv.at[b, s, k - 1], device))
        return out

    def fin_copy(b):
        return remote(fin_out.at[b], fin_in.at[b], fin_send.at[b], fin_recv.at[b], partner)

    def step_r(b):
        tile = jnp.zeros((16, 128), jnp.float32)
        for n, mat in enumerate(BATCHES[b]):
            s = slot_of(mat)
            if mat in GROUPED_MATS:
                i = GROUPED_MATS.index(mat)
                total = g_part[i, coords[AXIS_OF[mat]]]
                for k in range(1, RING):
                    g_copy(mat, k).wait_recv()
                    total = total + g_got[i, k - 1]
                g_all[s] = total
            grad = g_all[s]
            q_sq = grad * grad + EPS_SQUARE
            tile = jnp.where(lane == n, jnp.sum(q_sq, axis=1, keepdims=True), tile)
        pair_out[b] = tile
        pair_copy(b).start()

    def step_d(b):
        here = coords[0]
        mats = BATCHES[b]
        weights = [wo[mat[0]] if mat[1] == 3 else wq[mat[0], mat[1]] for mat in mats]
        w_sq = [jnp.sum(jnp.sum(w * w, axis=0, keepdims=True), axis=1, keepdims=True) for w in weights]
        q_col = []
        for mat in mats:
            grad = g_all[slot_of(mat)]
            q_col.append(jnp.sum(grad * grad + EPS_SQUARE, axis=0, keepdims=True))
        pair_copy(b).wait_recv()
        row_total = pair_out[b] + pair_in[b]
        for n, mat in enumerate(mats):
            layer, m = mat
            s = slot_of(mat)
            old = co[layer : layer + 1, :] if m == 3 else rq[m, layer : layer + 1, :]
            new = beta_two * up(old) + (1.0 - beta_two) * (row_total[:, n : n + 1] / width)
            if m == 3:
                co[layer : layer + 1, :] = across(new)
            else:
                rq[m, layer : layer + 1, :] = across(new)
            t = g_all[s] * lax.rsqrt(new)
            g_all[s] = t
            t_big = t * T_SCALE
            t_col = jnp.sum(t_big * t_big, axis=0, keepdims=True)
            stage[b, 0, here, n : n + 1, 0:512] = q_col[n]
            stage[b, 0, here, n : n + 1, 512:640] = jnp.broadcast_to(jnp.sum(new, axis=0, keepdims=True), (1, 128))
            stage[b, 0, here, 4 + n : 5 + n, 0:512] = t_col
            stage[b, 0, here, 4 + n : 5 + n, 512:640] = jnp.broadcast_to(w_sq[n], (1, 128))
        for n in range(len(mats), 4):
            stage[b, 0, here, n : n + 1, :] = jnp.zeros((1, 640), jnp.float32)
            stage[b, 0, here, 4 + n : 5 + n, :] = jnp.zeros((1, 640), jnp.float32)
        for copy in stage_copies(b, 0):
            copy.start()

    def gather(b, s):
        for copy in stage_copies(b, s):
            copy.wait_recv()
        return (stage[b, s, 0] + stage[b, s, 1]) + (stage[b, s, 2] + stage[b, s, 3])

    def step_s(b, s):
        stage[b, s, coords[s]] = gather(b, s - 1)
        for copy in stage_copies(b, s):
            copy.start()

    sums = {}

    def step_f(b):
        total = gather(b, 2)
        rows = [jnp.zeros((1, 128), jnp.float32)] * 16
        for n, mat in enumerate(BATCHES[b]):
            layer, m = mat
            old = ro[layer : layer + 1, :] if m == 3 else cq[m, layer : layer + 1, :]
            new = beta_two * old + (1.0 - beta_two) * (total[n : n + 1, 0:512] / width)
            if m == 3:
                ro[layer : layer + 1, :] = new
            else:
                cq[m, layer : layer + 1, :] = new
            v = (jnp.sqrt(total[4 + n : 5 + n, 0:512]) * (1.0 / T_SCALE)) * lax.rsqrt(new)
            rows[n] = jnp.broadcast_to(jnp.sum(v * v, axis=1, keepdims=True), (1, 128))
            rows[4 + n] = total[4 + n : 5 + n, 512:640]
            rows[8 + n] = (
                jnp.broadcast_to(jnp.sum(new, axis=1, keepdims=True), (1, 128)) if m == 3 else total[n : n + 1, 512:640] * 0.5
            )
        for i, row in enumerate(rows):
            fin_out[b, i : i + 1, :] = row
        fin_copy(b).start()

    def out_copies(b):
        out = []
        for mat in BATCHES[b]:
            layer, m = mat
            src, dst = (wo.at[layer], w_out_new.at[layer]) if m == 3 else (wq.at[layer, m], w_qkv_new.at[layer, m])
            out.append(pltpu.make_async_copy(src, dst, out_sem.at[slot_of(mat)]))
        return out

    def step_w(b):
        fin_copy(b).wait_recv()
        total = fin_out[b] + fin_in[b]
        for n, mat in enumerate(BATCHES[b]):
            layer, m = mat
            mean_row = total[8 + n : 9 + n, 0:1] / width
            rms_u = jnp.sqrt(mean_row * total[n : n + 1, 0:1] / n_elems)
            rms_w = jnp.sqrt(total[4 + n : 5 + n, 0:1] / n_elems)
            step_size = rel_step * jnp.maximum(EPS_SCALE, rms_w) / jnp.maximum(1.0, rms_u / clip_limit)
            factor = jnp.sqrt(mean_row) * step_size
            j_new = ro[layer : layer + 1, :] if m == 3 else cq[m, layer : layer + 1, :]
            update = (g_all[slot_of(mat)] * lax.rsqrt(j_new)) * factor
            if m == 3:
                wo[layer] = wo[layer] - update
            else:
                wq[layer, m] = wq[layer, m] - update
        for copy in out_copies(b):
            copy.start()

    waited = False
    for what, which in PLAN:
        if what == "U":
            products(which)
        elif what == "R":
            step_r(which)
        elif what == "D":
            if not waited:
                for copy in small:
                    copy.wait()
                waited = True
            step_d(which)
        elif what == "S1":
            step_s(which, 1)
        elif what == "S2":
            step_s(which, 2)
        elif what == "F":
            step_f(which)
        else:
            step_w(which)

    last = [
        pltpu.make_async_copy(src, dst, out_sem.at[16 + i])
        for i, (src, dst) in enumerate(((rq, r_qkv_new), (cq, c_qkv_new), (ro, r_out_new), (co, c_out_new)))
    ]
    for copy in last:
        copy.start()
    for b in range(len(BATCHES)):
        for copy in out_copies(b):
            copy.wait()
    for copy in last:
        copy.wait()
    for u in GROUPED:
        for k in range(1, RING):
            x_copy(u, k).wait_send()
    for mat in GROUPED_MATS:
        for k in range(1, RING):
            g_copy(mat, k).wait_send()
    for b in range(len(BATCHES)):
        pair_copy(b).wait_send()
        fin_copy(b).wait_send()
        for s in range(3):
            for copy in stage_copies(b, s):
                copy.wait_send()


def solution(mesh):
    emb_size = mesh.shape["emb"]
    att_size = mesh.shape["att"]
    in_specs = (
        P(None, None, "emb", "att"),
        P(None, "att", "emb"),
        P(None, None, "emb"),
        P(None, None, None, "att"),
        P(None, None, "att"),
        P(None, None, "emb"),
        P(None, None, "emb"),
        P(None, None, "att"),
        P(None, "att"),
        P(None, "emb"),
        P(),
    )
    out_specs = (
        P(None, None, "emb", "att"),
        P(None, "att", "emb"),
        P(None, None, "emb"),
        P(None, None, "att"),
        P(None, "att"),
        P(None, "emb"),
    )

    def local_run(w_qkv, w_out, x_in, dy_qkv, x_attn, dy_out, r_qkv, c_qkv, r_out, c_out, hyper_params):
        tokens, width = x_in.shape[1], x_in.shape[2] * emb_size
        part = tokens // RING
        w_out = jnp.swapaxes(w_out, 1, 2)
        x_in = jnp.swapaxes(x_in, 1, 2)
        dy_out = jnp.swapaxes(dy_out, 1, 2)
        r_qkv = jnp.swapaxes(r_qkv, 0, 1)
        c_qkv = jnp.swapaxes(c_qkv, 0, 1)
        f32, bf16 = jnp.float32, jnp.bfloat16
        cols = dy_qkv.shape[3]
        n_part, n_whole, n_b = len(GROUPED_MATS), len(WHOLE), len(BATCHES)
        dma = pltpu.SemaphoreType.DMA
        results = (w_qkv, w_out, r_qkv, c_qkv, r_out, c_out)
        out = pl.pallas_call(
            functools.partial(kernel, tokens, width, att_size),
            out_shape=tuple(jax.ShapeDtypeStruct(a.shape, a.dtype) for a in results),
            in_specs=[pl.BlockSpec(memory_space=pl.ANY)] * 10 + [pl.BlockSpec(memory_space=pltpu.SMEM)],
            out_specs=tuple(pl.BlockSpec(memory_space=pl.ANY) for _ in results),
            scratch_shapes=[
                pltpu.VMEM((n_part, part, cols), bf16),
                pltpu.VMEM((n_whole, tokens, cols), bf16),
                pltpu.VMEM((len(GROUPED), RING, 16, part), bf16),
                pltpu.VMEM((n_whole, 16, tokens), bf16),
                pltpu.VMEM((n_part, RING, 16, cols), f32),
                pltpu.VMEM((n_part, RING - 1, 16, cols), f32),
                pltpu.VMEM((16, 16, cols), f32),
                pltpu.VMEM(w_qkv.shape, f32),
                pltpu.VMEM(w_out.shape, f32),
                pltpu.VMEM(r_qkv.shape, f32),
                pltpu.VMEM(c_qkv.shape, f32),
                pltpu.VMEM(r_out.shape, f32),
                pltpu.VMEM(c_out.shape, f32),
                pltpu.VMEM((n_b, 16, 128), f32),
                pltpu.VMEM((n_b, 16, 128), f32),
                pltpu.VMEM((n_b, 3, RING, 8, cols + 128), f32),
                pltpu.VMEM((n_b, 16, 128), f32),
                pltpu.VMEM((n_b, 16, 128), f32),
                dma((6,)),
                dma((len(UNITS),)),
                dma((n_part + n_whole * RING,)),
                dma((len(GROUPED), RING - 1)),
                dma((len(GROUPED), RING - 1)),
                dma((n_part, RING - 1)),
                dma((n_part, RING - 1)),
                dma((n_b,)),
                dma((n_b,)),
                dma((n_b, 3, RING - 1)),
                dma((n_b, 3, RING - 1)),
                dma((n_b,)),
                dma((n_b,)),
                dma((20,)),
            ],
            compiler_params=pltpu.CompilerParams(
                collective_id=0, has_side_effects=True, vmem_limit_bytes=64 * 1024 * 1024 - 64 * 1024
            ),
            name="adafactor",
        )(w_qkv, w_out, x_in, dy_qkv, x_attn, dy_out, r_qkv, c_qkv, r_out, c_out, hyper_params)
        return (
            out[0],
            jnp.swapaxes(out[1], 1, 2),
            jnp.swapaxes(out[2], 0, 1),
            jnp.swapaxes(out[3], 0, 1),
            out[4],
            out[5],
        )

    return jax.shard_map(local_run, mesh=mesh, in_specs=in_specs, out_specs=out_specs, check_vma=False)
```

time: 722 us -> 69.9 us (0.10)
  blocking collectives: 604 us -> 0 us
  matrix products: 61.2 us -> 0 us
  Pallas kernels: 0 us -> 60.4 us
  other arithmetic: 27.9 us -> 0 us
  between operations: 22.6 us -> 0.65 us
    psum x6 -> x0, blocking collectives: 604 us -> none  [the longest x1 290 us: factored_step(): col_sum = lax.psum(col_part, m_axis)]
    dot_general x8 -> x0, matrix products: 61.2 us -> none  [the longest x4 40.1 us: local_run(): jnp.einsum('td,ktn->kdn', x_in[layer_idx], dy_qkv[layer_idx], preferred_e...]
    pallas_call x0 -> x1, Pallas kernels: none -> 60.4 us  [local_run(): pl.pallas_call(functools.partial(kernel, tokens, width, att_size), out_sh...]
    another operation x23 -> x0, other arithmetic: 10.5 us -> none  [the longest x8 5.39 us: factored_step(): jnp.stack([jnp.sum(col_part, axis=1), jnp.sum(weight * weight, axis=(1, 2...]
    reduce_sum x11 -> x0, other arithmetic: 7.73 us -> none  [the longest x8 3.57 us: factored_step(): u_sum = lax.psum(jnp.sum(update * update, axis=(1, 2)), (m_axis, n_axis))]
    unnamed x12 -> x6, local copies, waits for them, and re-layouts: 1.26 us -> 8.51 us
where the time goes in v1:
time: 69.9 us; the launch traced here: 69.6 us
  Pallas kernels  60.4 us (86%)
  local copies, waits for them, and re-layouts  8.51 us (12%)
    pallas_call x1, Pallas kernels, local_run(): pl.pallas_call(functools.partial(kernel, tokens, width, att_size), out_sh...  60.4 us
    unnamed x6, local copies, waits for them, and re-layouts  8.51 us

profile of v1, /device:TPU:1, one launch (start us, length us, event | category | flops | bytes accessed | tf_op | source)
XLA Modules:
  0.0 69.6 jit_solution(3590419014176831800)
XLA Ops:
  0.6 60.4 %adafactor.1 = (f32[4,3,16,512]{3,2,1,0:T(8,128)}, f32[4,16,512]{2,1,0:T(8,128)}, f32[3,4,16]{2,1,0:T(4,128)}, f32[3,4,512]{2,1,0:T(4,128)}, f32[4,512]{1,0:T(4,128)}, /*index=5*/f32[4,16]{1,0:T(4,128)}) custom-call(f32[4,3,16,512]{3,2,1,0:T(8,128)} %w_qkv.1, f32[4,16,512]{2,1,0:T(8,128)} %bitcast.10, bf16[4,16,8192]{2,1,0:T(8,128)(2,1)} %bitcast.8, ...), custom_call_target="tpu_custom_call" | custom-call | tf_op jit(solution)/shard_map/adafactor/pallas_call | solution.py:402
  61.1 1.8 %copy.23 = f32[4,3,16,512]{3,2,1,0:T(8,128)} copy(f32[4,3,16,512]{3,2,1,0:T(8,128)} %get-tuple-element.24) | data formatting | bytes 786432
  62.8 1.6 %copy.24 = f32[4,512,16]{1,2,0:T(8,128)} copy(f32[4,512,16]{1,2,0:T(8,128)} %bitcast.11) | data formatting | bytes 262144
  64.4 1.3 %copy.25 = f32[4,3,16]{2,0,1:T(4,128)} copy(f32[4,3,16]{2,0,1:T(4,128)} %bitcast.15) | data formatting | bytes 1536
  65.7 1.3 %copy.26 = f32[4,3,512]{2,0,1:T(4,128)} copy(f32[4,3,512]{2,0,1:T(4,128)} %bitcast.13) | data formatting | bytes 49152
  67.0 1.3 %copy.27 = f32[4,512]{1,0:T(4,128)} copy(f32[4,512]{1,0:T(4,128)} %get-tuple-element.28) | data formatting | bytes 16384
  68.3 1.3 %copy.28 = f32[4,16]{1,0:T(4,128)} copy(f32[4,16]{1,0:T(4,128)} %get-tuple-element.29) | data formatting | bytes 512

commit v2 on v1

--- a/solution.py
+++ b/solution.py
@@ -39,6 +39,9 @@
     ("W", 1), ("F", 2), ("S2", 3), ("S1", 4), ("W", 2), ("F", 3), ("S2", 4), ("W", 3), ("F", 4), ("W", 4),
 )
 
+AHEAD_FIRST = 10
+AHEAD = 4
+
 GROUPED = tuple(u for u, unit in enumerate(UNITS) if unit[2] is not None)
 WHOLE = tuple(u for u, unit in enumerate(UNITS) if unit[2] is None)
 
@@ -56,7 +59,7 @@
     tokens, width, att_size,
     w_qkv, w_out, x_in, dy_qkv, x_attn, dy_out, r_qkv, c_qkv, r_out, c_out, hyper,
     w_qkv_new, w_out_new, r_qkv_new, c_qkv_new, r_out_new, c_out_new,
-    dy_part, dy_whole, x_part, x_whole, g_part, g_got, g_all, wq, wo, rq, cq, ro, co,
+    dy_part, dy_whole, x_full, x_part, g_part, g_got, g_all, wq, wo, rq, cq, ro, co,
     pair_out, pair_in, stage, fin_out, fin_in,
     small_sem, own_sem, dy_sem, x_send, x_recv, g_send, g_recv, pair_send, pair_recv, st_send, st_recv, fin_send, fin_recv,
     out_sem,
@@ -85,25 +88,19 @@
             ((w_qkv, wq), (w_out, wo), (r_qkv, rq), (c_qkv, cq), (r_out, ro), (c_out, co))
         )
     ]
-    for copy in small:
-        copy.start()
 
     def x_source(u):
         layer, kind, _ = UNITS[u]
         return (x_in, dy_out)[kind].at[layer]
 
     def x_own(u):
-        if u in GROUPED:
-            here = coords[UNITS[u][2]]
-            src = x_source(u).at[:, pl.ds(pl.multiple_of(here * part, part), part)]
-            return pltpu.make_async_copy(src, x_part.at[GROUPED.index(u), here], own_sem.at[u])
-        return pltpu.make_async_copy(x_source(u), x_whole.at[WHOLE.index(u)], own_sem.at[u])
+        return pltpu.make_async_copy(x_source(u), x_full.at[u], own_sem.at[u])
 
     def x_copy(u, k):
         axis = UNITS[u][2]
         device, there = peer(axis, k)
         slot = GROUPED.index(u)
-        src = x_source(u).at[:, pl.ds(pl.multiple_of(there * part, part), part)]
+        src = x_full.at[u, :, pl.ds(pl.multiple_of(there * part, part), part)]
         return remote(src, x_part.at[slot, coords[axis]], x_send.at[slot, k - 1], x_recv.at[slot, k - 1], device)
 
     def dy_source(mat):
@@ -131,8 +128,17 @@
 
     for u in range(len(UNITS)):
         x_own(u).start()
-        for copy in dy_copies(u):
+    for copy in small:
+        copy.start()
+    loads = [copy for u in range(len(UNITS)) for copy in dy_copies(u)]
+    started = [0]
+
+    def start_loads(upto):
+        for copy in loads[started[0] : upto]:
             copy.start()
+        started[0] = max(started[0], min(upto, len(loads)))
+
+    start_loads(AHEAD_FIRST)
 
     barrier = pltpu.get_barrier_semaphore()
     neighbours = [peer(axis, k)[0] for axis in (X, Y, Z) for k in range(1, RING)] + [partner]
@@ -140,9 +146,13 @@
         pl.semaphore_signal(barrier, inc=1, device_id=device, device_id_type=pl.DeviceIdType.MESH)
     pl.semaphore_wait(barrier, len(neighbours))
 
-    for u in GROUPED:
-        for k in (1, 3, 2):
-            x_copy(u, k).start()
+    for u in range(len(UNITS)):
+        x_own(u).wait()
+        if u in GROUPED:
+            for k in (1, 3, 2):
+                x_copy(u, k).start()
+            here = coords[UNITS[u][2]]
+            x_part[GROUPED.index(u), here] = x_full[u, :, pl.ds(pl.multiple_of(here * part, part), part)]
 
     def g_copy(mat, k):
         axis = AXIS_OF[mat]
@@ -153,8 +163,9 @@
     def slot_of(mat):
         return mat[0] * 4 + mat[1]
 
+    done = [0]
+
     def products(u):
-        x_own(u).wait()
         copies = dy_copies(u)
         if u in GROUPED:
             for k in range(1, RING):
@@ -163,6 +174,8 @@
             for mat, copy in zip(mats_of(UNITS[u]), copies):
                 i = GROUPED_MATS.index(mat)
                 copy.wait()
+                done[0] += 1
+                start_loads(done[0] + AHEAD)
                 got = jnp.dot(
                     lhs[...].reshape(RING * 16, part), dy_part[i], preferred_element_type=jnp.float32
                 )
@@ -175,8 +188,10 @@
             total = None
             for j, copy in enumerate(copies):
                 copy.wait()
+                done[0] += 1
+                start_loads(done[0] + AHEAD)
                 rows = pl.ds(j * part, part)
-                got = jnp.dot(x_whole[w, :, rows], dy_whole[w, rows, :], preferred_element_type=jnp.float32)
+                got = jnp.dot(x_full[u, :, rows], dy_whole[w, rows, :], preferred_element_type=jnp.float32)
                 total = got if total is None else total + got
             g_all[slot_of(mat)] = total
 
@@ -361,6 +376,18 @@
                 copy.wait_send()
 
 
+def emit(*refs):
+    n = len(refs) // 3
+    ins, outs, bufs, sem = refs[:n], refs[n : 2 * n], refs[2 * n : 3 * n], refs[-1]
+    for i in range(n):
+        pltpu.make_async_copy(ins[i], bufs[i], sem.at[0, i]).start()
+    for i in range(n):
+        pltpu.make_async_copy(ins[i], bufs[i], sem.at[0, i]).wait()
+        pltpu.make_async_copy(bufs[i], outs[i], sem.at[1, i]).start()
+    for i in range(n):
+        pltpu.make_async_copy(bufs[i], outs[i], sem.at[1, i]).wait()
+
+
 def solution(mesh):
     emb_size = mesh.shape["emb"]
     att_size = mesh.shape["att"]
@@ -407,8 +434,8 @@
             scratch_shapes=[
                 pltpu.VMEM((n_part, part, cols), bf16),
                 pltpu.VMEM((n_whole, tokens, cols), bf16),
+                pltpu.VMEM((len(UNITS), 16, tokens), bf16),
                 pltpu.VMEM((len(GROUPED), RING, 16, part), bf16),
-                pltpu.VMEM((n_whole, 16, tokens), bf16),
                 pltpu.VMEM((n_part, RING, 16, cols), f32),
                 pltpu.VMEM((n_part, RING - 1, 16, cols), f32),
                 pltpu.VMEM((16, 16, cols), f32),
@@ -443,6 +470,14 @@
             ),
             name="adafactor",
         )(w_qkv, w_out, x_in, dy_qkv, x_attn, dy_out, r_qkv, c_qkv, r_out, c_out, hyper_params)
+        out = pl.pallas_call(
+            emit,
+            out_shape=tuple(jax.ShapeDtypeStruct(a.shape, a.dtype) for a in out),
+            in_specs=[pl.BlockSpec(memory_space=pl.ANY)] * len(out),
+            out_specs=tuple(pl.BlockSpec(memory_space=pl.ANY) for _ in out),
+            scratch_shapes=[pltpu.VMEM(a.shape, a.dtype) for a in out] + [dma((2, len(out)))],
+            name="emit",
+        )(*out)
         return (
             out[0],
             jnp.swapaxes(out[1], 1, 2),

time: 69.9 us -> 61.8 us (0.88)
  local copies, waits for them, and re-layouts: 8.51 us -> 0 us
    unnamed x6 -> x0, local copies, waits for them, and re-layouts: 8.51 us -> none
    pallas_call x0 -> x1, Pallas kernels: none -> 1.89 us  [local_run(): pl.pallas_call(emit, out_shape=tuple((jax.ShapeDtypeStruct(a.shape, a.dty...]
    pallas_call x1, Pallas kernels: 60.4 us -> 59.2 us  [local_run(): pl.pallas_call(functools.partial(kernel, tokens, width, att_size), out_sh...]
where the time goes in v2:
time: 61.8 us; the launch traced here: 61.7 us
  Pallas kernels  61 us (99%)
  between operations  0.64 us (1%)
    pallas_call x1, Pallas kernels, local_run(): pl.pallas_call(functools.partial(kernel, tokens, width, att_size), out_sh...  59.2 us
    pallas_call x1, Pallas kernels, local_run(): pl.pallas_call(emit, out_shape=tuple((jax.ShapeDtypeStruct(a.shape, a.dty...  1.89 us

profile of v2, /device:TPU:1, one launch (start us, length us, event | category | flops | bytes accessed | tf_op | source)
XLA Modules:
  0.0 61.7 jit_solution(15473148767418659504)
XLA Ops:
  0.6 59.2 %adafactor.1 = (f32[4,3,16,512]{3,2,1,0:T(8,128)}, f32[4,16,512]{2,1,0:T(8,128)}, f32[3,4,16]{2,1,0:T(4,128)}, f32[3,4,512]{2,1,0:T(4,128)}, f32[4,512]{1,0:T(4,128)}, /*index=5*/f32[4,16]{1,0:T(4,128)}) custom-call(f32[4,3,16,512]{3,2,1,0:T(8,128)} %w_qkv.1, f32[4,16,512]{2,1,0:T(8,128)} %bitcast.10, bf16[4,16,8192]{2,1,0:T(8,128)(2,1)} %bitcast.8, ...), custom_call_target="tpu_custom_call" | custom-call | tf_op jit(solution)/shard_map/adafactor/pallas_call | solution.py:429
  59.8 1.9 %emit.1 = (f32[4,3,16,512]{3,2,1,0:T(8,128)}, f32[4,16,512]{2,1,0:T(8,128)}, f32[3,4,16]{2,1,0:T(4,128)}, f32[3,4,512]{2,1,0:T(4,128)}, f32[4,512]{1,0:T(4,128)}, /*index=5*/f32[4,16]{1,0:T(4,128)}) custom-call(f32[4,3,16,512]{3,2,1,0:T(8,128)} %get-tuple-element.18.refs_0_, f32[4,16,512]{2,1,0:T(8,128)} %get-tuple-element.19.refs_1_, ...), custom_call_target="tpu_custom_call" | custom-call | tf_op jit(solution)/shard_map/emit/pallas_call | solution.py:473

commit v3 on v2

--- a/solution.py
+++ b/solution.py
@@ -15,28 +15,31 @@
 X, Y, Z = 0, 1, 2
 STRIDES = (1, 4, 16)
 
+SQUARES = (((X, 0), (Y, 0)), ((Y, 1), (Z, 0)), ((Z, 1), (X, 1)))
 UNITS = (
-    (0, 0, X),
-    (0, 1, Y),
-    (1, 0, Y),
-    (1, 1, Z),
-    (2, 0, Z),
-    (3, 0, X),
+    (0, 0, 0),
+    (1, 0, 1),
+    (2, 0, 2),
+    (3, 0, 0),
+    (0, 1, 1),
+    (1, 1, 2),
     (2, 1, None),
     (3, 1, None),
 )
 BATCHES = (
-    ((0, 0), (0, 1), (0, 2), (0, 3)),
-    ((1, 0), (1, 1), (1, 2), (1, 3)),
+    ((0, 0), (0, 1), (0, 2)),
+    ((1, 0), (1, 1), (1, 2)),
     ((2, 0), (2, 1), (2, 2)),
-    ((3, 0), (3, 1), (3, 2), (2, 3)),
+    ((3, 0), (3, 1), (3, 2), (0, 3)),
+    ((1, 3), (2, 3)),
     ((3, 3),),
 )
 PLAN = (
-    ("U", 0), ("U", 1), ("U", 2), ("R", 0), ("U", 3), ("D", 0), ("U", 4), ("R", 1), ("S1", 0), ("U", 5), ("D", 1),
-    ("R", 2), ("S2", 0), ("S1", 1), ("D", 2), ("U", 6), ("R", 3), ("F", 0), ("S2", 1), ("S1", 2), ("D", 3),
-    ("U", 7), ("R", 4), ("W", 0), ("F", 1), ("S2", 2), ("S1", 3), ("D", 4),
-    ("W", 1), ("F", 2), ("S2", 3), ("S1", 4), ("W", 2), ("F", 3), ("S2", 4), ("W", 3), ("F", 4), ("W", 4),
+    ("U", 0), ("U", 1), ("U", 2), ("R", 0), ("U", 3), ("D", 0), ("R", 1), ("U", 4), ("S1", 0), ("D", 1), ("R", 2), ("U", 5),
+    ("S2", 0), ("S1", 1), ("D", 2), ("U", 6), ("R", 3), ("F", 0), ("S2", 1), ("S1", 2), ("D", 3),
+    ("R", 4), ("U", 7), ("R", 5), ("W", 0), ("F", 1), ("S2", 2), ("D", 4), ("S1", 3), ("D", 5),
+    ("W", 1), ("F", 2), ("S1", 4), ("S2", 3), ("S1", 5), ("W", 2), ("F", 3), ("S2", 4), ("S2", 5),
+    ("W", 3), ("F", 4), ("F", 5), ("W", 4), ("W", 5),
 )
 
 AHEAD_FIRST = 10
@@ -52,7 +55,7 @@
 
 
 GROUPED_MATS = tuple(mat for u in GROUPED for mat in mats_of(UNITS[u]))
-AXIS_OF = {mat: UNITS[u][2] for u in GROUPED for mat in mats_of(UNITS[u])}
+SQUARE_OF = {mat: UNITS[u][2] for u in GROUPED for mat in mats_of(UNITS[u])}
 
 
 def kernel(
@@ -60,7 +63,7 @@
     w_qkv, w_out, x_in, dy_qkv, x_attn, dy_out, r_qkv, c_qkv, r_out, c_out, hyper,
     w_qkv_new, w_out_new, r_qkv_new, c_qkv_new, r_out_new, c_out_new,
     dy_part, dy_whole, x_full, x_part, g_part, g_got, g_all, wq, wo, rq, cq, ro, co,
-    pair_out, pair_in, stage, fin_out, fin_in,
+    pair_out, pair_in, stage, fin_out, fin_in, w_total,
     small_sem, own_sem, dy_sem, x_send, x_recv, g_send, g_recv, pair_send, pair_recv, st_send, st_recv, fin_send, fin_recv,
     out_sem,
 ):
@@ -75,6 +78,23 @@
         place = lax.rem(coords[axis] + k, RING)
         return (att, emb + (place - coords[axis]) * STRIDES[axis]), place
 
+    def bit(axis, first):
+        return lax.rem(coords[axis] + first, 2)
+
+    def place_in(square):
+        (axis_a, first_a), (axis_b, first_b) = SQUARES[square]
+        return bit(axis_a, first_a) + 2 * bit(axis_b, first_b)
+
+    def mate(square, k):
+        index, place = emb, place_in(square)
+        for n, (axis, first) in enumerate(SQUARES[square]):
+            if k & (1 << n):
+                here = bit(axis, first)
+                there = lax.rem(coords[axis] + RING + 1 - 2 * here, RING)
+                index = index + (there - coords[axis]) * STRIDES[axis]
+                place = place + (1 - 2 * here) * (1 << n)
+        return (att, index), place
+
     partner = (lax.rem(att + 1, att_size), emb)
 
     def remote(src, dst, send, recv, device):
@@ -97,11 +117,11 @@
         return pltpu.make_async_copy(x_source(u), x_full.at[u], own_sem.at[u])
 
     def x_copy(u, k):
-        axis = UNITS[u][2]
-        device, there = peer(axis, k)
+        square = UNITS[u][2]
+        device, there = mate(square, k)
         slot = GROUPED.index(u)
         src = x_full.at[u, :, pl.ds(pl.multiple_of(there * part, part), part)]
-        return remote(src, x_part.at[slot, coords[axis]], x_send.at[slot, k - 1], x_recv.at[slot, k - 1], device)
+        return remote(src, x_part.at[slot, place_in(square)], x_send.at[slot, k - 1], x_recv.at[slot, k - 1], device)
 
     def dy_source(mat):
         layer, m = mat
@@ -112,7 +132,7 @@
         for mat in mats_of(UNITS[u]):
             if u in GROUPED:
                 i = GROUPED_MATS.index(mat)
-                here = coords[UNITS[u][2]]
+                here = place_in(UNITS[u][2])
                 src = dy_source(mat).at[pl.ds(pl.multiple_of(here * part, part), part), :]
                 out.append(pltpu.make_async_copy(src, dy_part.at[i], dy_sem.at[i]))
             else:
@@ -142,6 +162,7 @@
 
     barrier = pltpu.get_barrier_semaphore()
     neighbours = [peer(axis, k)[0] for axis in (X, Y, Z) for k in range(1, RING)] + [partner]
+    neighbours += [mate(square, 3)[0] for square in range(len(SQUARES))]
     for device in neighbours:
         pl.semaphore_signal(barrier, inc=1, device_id=device, device_id_type=pl.DeviceIdType.MESH)
     pl.semaphore_wait(barrier, len(neighbours))
@@ -149,14 +170,13 @@
     for u in range(len(UNITS)):
         x_own(u).wait()
         if u in GROUPED:
-            for k in (1, 3, 2):
+            for k in (3, 1, 2):
                 x_copy(u, k).start()
-            here = coords[UNITS[u][2]]
+            here = place_in(UNITS[u][2])
             x_part[GROUPED.index(u), here] = x_full[u, :, pl.ds(pl.multiple_of(here * part, part), part)]
 
     def g_copy(mat, k):
-        axis = AXIS_OF[mat]
-        device, there = peer(axis, k)
+        device, there = mate(SQUARE_OF[mat], k)
         i = GROUPED_MATS.index(mat)
         return remote(g_part.at[i, there], g_got.at[i, k - 1], g_send.at[i, k - 1], g_recv.at[i, k - 1], device)
 
@@ -212,7 +232,7 @@
         out = []
         for k in range(1, RING):
             device, _ = peer(s, k)
-            slot = stage.at[b, s, here]
+            slot = stage.at[b, s, here, 0 : rows_of(b), :]
             out.append(remote(slot, slot, st_send.at[b, s, k - 1], st_recv.at[b, s, k - 1], device))
         return out
 
@@ -225,7 +245,7 @@
             s = slot_of(mat)
             if mat in GROUPED_MATS:
                 i = GROUPED_MATS.index(mat)
-                total = g_part[i, coords[AXIS_OF[mat]]]
+                total = g_part[i, place_in(SQUARE_OF[mat])]
                 for k in range(1, RING):
                     g_copy(mat, k).wait_recv()
                     total = total + g_got[i, k - 1]
@@ -236,17 +256,26 @@
         pair_out[b] = tile
         pair_copy(b).start()
 
+    def rows_of(b):
+        return 8 * len(BATCHES[b]) + (0 if b == len(BATCHES) - 1 else 8)
+
     def step_d(b):
         here = coords[0]
         mats = BATCHES[b]
-        weights = [wo[mat[0]] if mat[1] == 3 else wq[mat[0], mat[1]] for mat in mats]
-        w_sq = [jnp.sum(jnp.sum(w * w, axis=0, keepdims=True), axis=1, keepdims=True) for w in weights]
         q_col = []
         for mat in mats:
             grad = g_all[slot_of(mat)]
             q_col.append(jnp.sum(grad * grad + EPS_SQUARE, axis=0, keepdims=True))
+        if b == 0:
+            w_sq = jnp.zeros((1, 128), jnp.float32)
+            for layer in range(4):
+                for m in range(4):
+                    w = wo[layer] if m == 3 else wq[layer, m]
+                    w_sum = jnp.sum(jnp.sum(w * w, axis=0, keepdims=True), axis=1, keepdims=True)
+                    w_sq = jnp.where(lane[0:1] == layer * 4 + m, w_sum, w_sq)
         pair_copy(b).wait_recv()
         row_total = pair_out[b] + pair_in[b]
+        out = stage.at[b, 0, here]
         for n, mat in enumerate(mats):
             layer, m = mat
             s = slot_of(mat)
@@ -260,47 +289,57 @@
             g_all[s] = t
             t_big = t * T_SCALE
             t_col = jnp.sum(t_big * t_big, axis=0, keepdims=True)
-            stage[b, 0, here, n : n + 1, 0:512] = q_col[n]
-            stage[b, 0, here, n : n + 1, 512:640] = jnp.broadcast_to(jnp.sum(new, axis=0, keepdims=True), (1, 128))
-            stage[b, 0, here, 4 + n : 5 + n, 0:512] = t_col
-            stage[b, 0, here, 4 + n : 5 + n, 512:640] = jnp.broadcast_to(w_sq[n], (1, 128))
-        for n in range(len(mats), 4):
-            stage[b, 0, here, n : n + 1, :] = jnp.zeros((1, 640), jnp.float32)
-            stage[b, 0, here, 4 + n : 5 + n, :] = jnp.zeros((1, 640), jnp.float32)
+            for i in range(4):
+                lanes = slice(128 * i, 128 * i + 128)
+                out[8 * n + i : 8 * n + i + 1, :] = q_col[n][:, lanes]
+                out[8 * n + 4 + i : 8 * n + 5 + i, :] = t_col[:, lanes]
+            if b < len(BATCHES) - 1:
+                last = 8 * len(mats) + n
+                out[last : last + 1, :] = jnp.broadcast_to(jnp.sum(new, axis=0, keepdims=True), (1, 128))
+        if b < len(BATCHES) - 1:
+            for n in range(len(mats), 8):
+                last = 8 * len(mats) + n
+                out[last : last + 1, :] = w_sq if b == 0 and n == 4 else jnp.zeros((1, 128), jnp.float32)
         for copy in stage_copies(b, 0):
             copy.start()
 
     def gather(b, s):
         for copy in stage_copies(b, s):
             copy.wait_recv()
-        return (stage[b, s, 0] + stage[b, s, 1]) + (stage[b, s, 2] + stage[b, s, 3])
+        part_0, part_1, part_2, part_3 = (stage[b, s, i, 0 : rows_of(b), :] for i in range(RING))
+        return (part_0 + part_1) + (part_2 + part_3)
 
     def step_s(b, s):
-        stage[b, s, coords[s]] = gather(b, s - 1)
+        stage[b, s, coords[s], 0 : rows_of(b), :] = gather(b, s - 1)
         for copy in stage_copies(b, s):
             copy.start()
 
-    sums = {}
-
     def step_f(b):
         total = gather(b, 2)
-        rows = [jnp.zeros((1, 128), jnp.float32)] * 16
-        for n, mat in enumerate(BATCHES[b]):
+        mats = BATCHES[b]
+        for n, mat in enumerate(mats):
             layer, m = mat
             old = ro[layer : layer + 1, :] if m == 3 else cq[m, layer : layer + 1, :]
-            new = beta_two * old + (1.0 - beta_two) * (total[n : n + 1, 0:512] / width)
+            q_col, t_col = (
+                jnp.concatenate([total[8 * n + 4 * h + i : 8 * n + 4 * h + i + 1, :] for i in range(4)], axis=1)
+                for h in range(2)
+            )
+            new = beta_two * old + (1.0 - beta_two) * (q_col / width)
             if m == 3:
                 ro[layer : layer + 1, :] = new
+                mean_part = jnp.sum(new, axis=1, keepdims=True)
             else:
                 cq[m, layer : layer + 1, :] = new
-            v = (jnp.sqrt(total[4 + n : 5 + n, 0:512]) * (1.0 / T_SCALE)) * lax.rsqrt(new)
-            rows[n] = jnp.broadcast_to(jnp.sum(v * v, axis=1, keepdims=True), (1, 128))
-            rows[4 + n] = total[4 + n : 5 + n, 512:640]
-            rows[8 + n] = (
-                jnp.broadcast_to(jnp.sum(new, axis=1, keepdims=True), (1, 128)) if m == 3 else total[n : n + 1, 512:640] * 0.5
-            )
-        for i, row in enumerate(rows):
-            fin_out[b, i : i + 1, :] = row
+                mean_part = total[8 * len(mats) + n : 8 * len(mats) + n + 1, 0:1] * 0.5
+            v = (jnp.sqrt(t_col) * (1.0 / T_SCALE)) * lax.rsqrt(new)
+            fin_out[b, n : n + 1, :] = jnp.broadcast_to(jnp.sum(v * v, axis=1, keepdims=True), (1, 128))
+            fin_out[b, 4 + n : 5 + n, :] = jnp.broadcast_to(mean_part, (1, 128))
+        for n in range(len(mats), 4):
+            fin_out[b, n : n + 1, :] = jnp.zeros((1, 128), jnp.float32)
+            fin_out[b, 4 + n : 5 + n, :] = jnp.zeros((1, 128), jnp.float32)
+        fin_out[b, 8:16, :] = jnp.zeros((8, 128), jnp.float32)
+        if b == 0:
+            fin_out[b, 8:9, :] = total[8 * len(mats) + 4 : 8 * len(mats) + 5, :]
         fin_copy(b).start()
 
     def out_copies(b):
@@ -314,11 +353,13 @@
     def step_w(b):
         fin_copy(b).wait_recv()
         total = fin_out[b] + fin_in[b]
+        if b == 0:
+            w_total[...] = total[8:16]
         for n, mat in enumerate(BATCHES[b]):
             layer, m = mat
-            mean_row = total[8 + n : 9 + n, 0:1] / width
+            mean_row = total[4 + n : 5 + n, 0:1] / width
             rms_u = jnp.sqrt(mean_row * total[n : n + 1, 0:1] / n_elems)
-            rms_w = jnp.sqrt(total[4 + n : 5 + n, 0:1] / n_elems)
+            rms_w = jnp.sqrt(w_total[0:1, slot_of(mat) : slot_of(mat) + 1] / n_elems)
             step_size = rel_step * jnp.maximum(EPS_SCALE, rms_w) / jnp.maximum(1.0, rms_u / clip_limit)
             factor = jnp.sqrt(mean_row) * step_size
             j_new = ro[layer : layer + 1, :] if m == 3 else cq[m, layer : layer + 1, :]
@@ -447,9 +488,10 @@
                 pltpu.VMEM(c_out.shape, f32),
                 pltpu.VMEM((n_b, 16, 128), f32),
                 pltpu.VMEM((n_b, 16, 128), f32),
-                pltpu.VMEM((n_b, 3, RING, 8, cols + 128), f32),
+                pltpu.VMEM((n_b, 3, RING, 40, 128), f32),
                 pltpu.VMEM((n_b, 16, 128), f32),
                 pltpu.VMEM((n_b, 16, 128), f32),
+                pltpu.VMEM((8, 128), f32),
                 dma((6,)),
                 dma((len(UNITS),)),
                 dma((n_part + n_whole * RING,)),

time: 61.8 us -> 59.5 us (0.963)
  Pallas kernels: 61 us -> 58.8 us
    pallas_call x1, Pallas kernels: 59.2 us -> 56.9 us  [local_run(): pl.pallas_call(functools.partial(kernel, tokens, width, att_size), out_sh...]
where the time goes in v3:
time: 59.5 us; the launch traced here: 59.4 us
  Pallas kernels  58.8 us (99%)
  between operations  0.64 us (1%)
    pallas_call x1, Pallas kernels, local_run(): pl.pallas_call(functools.partial(kernel, tokens, width, att_size), out_sh...  56.9 us
    pallas_call x1, Pallas kernels, local_run(): pl.pallas_call(emit, out_shape=tuple((jax.ShapeDtypeStruct(a.shape, a.dty...  1.89 us

profile of v3, /device:TPU:1, one launch (start us, length us, event | category | flops | bytes accessed | tf_op | source)
XLA Modules:
  0.0 59.4 jit_solution(14780498952204795978)
XLA Ops:
  0.6 56.9 %adafactor.1 = (f32[4,3,16,512]{3,2,1,0:T(8,128)}, f32[4,16,512]{2,1,0:T(8,128)}, f32[3,4,16]{2,1,0:T(4,128)}, f32[3,4,512]{2,1,0:T(4,128)}, f32[4,512]{1,0:T(4,128)}, /*index=5*/f32[4,16]{1,0:T(4,128)}) custom-call(f32[4,3,16,512]{3,2,1,0:T(8,128)} %w_qkv.1, f32[4,16,512]{2,1,0:T(8,128)} %bitcast.10, bf16[4,16,8192]{2,1,0:T(8,128)(2,1)} %bitcast.8, ...), custom_call_target="tpu_custom_call" | custom-call | tf_op jit(solution)/shard_map/adafactor/pallas_call | solution.py:470
  57.5 1.9 %emit.1 = (f32[4,3,16,512]{3,2,1,0:T(8,128)}, f32[4,16,512]{2,1,0:T(8,128)}, f32[3,4,16]{2,1,0:T(4,128)}, f32[3,4,512]{2,1,0:T(4,128)}, f32[4,512]{1,0:T(4,128)}, /*index=5*/f32[4,16]{1,0:T(4,128)}) custom-call(f32[4,3,16,512]{3,2,1,0:T(8,128)} %get-tuple-element.18.refs_0_, f32[4,16,512]{2,1,0:T(8,128)} %get-tuple-element.19.refs_1_, ...), custom_call_target="tpu_custom_call" | custom-call | tf_op jit(solution)/shard_map/emit/pallas_call | solution.py:515

commit v4 on v3

--- a/solution.py
+++ b/solution.py
@@ -17,32 +17,31 @@
 
 SQUARES = (((X, 0), (Y, 0)), ((Y, 1), (Z, 0)), ((Z, 1), (X, 1)))
 UNITS = (
-    (0, 0, 0),
-    (1, 0, 1),
-    (2, 0, 2),
-    (3, 0, 0),
-    (0, 1, 1),
-    (1, 1, 2),
-    (2, 1, None),
-    (3, 1, None),
+    (0, (0, 1, 2), 0),
+    (1, (0, 1, 2), 1),
+    (2, (0, 1, 2), 2),
+    (3, (0,), 0),
+    (3, (1,), 1),
+    (3, (2,), 2),
+    (0, (3,), 0),
+    (1, (3,), 1),
+    (2, (3,), None),
+    (3, (3,), None),
 )
 BATCHES = (
-    ((0, 0), (0, 1), (0, 2)),
-    ((1, 0), (1, 1), (1, 2)),
-    ((2, 0), (2, 1), (2, 2)),
-    ((3, 0), (3, 1), (3, 2), (0, 3)),
-    ((1, 3), (2, 3)),
-    ((3, 3),),
+    ((0, 0), (0, 1), (0, 2), (1, 0), (1, 1), (1, 2)),
+    ((2, 0), (2, 1), (2, 2), (3, 0), (2, 3), (3, 3)),
+    ((3, 1), (3, 2), (0, 3), (1, 3)),
 )
+AXES = ((X, Y, Z), (Y, Z, X), (Z, X, Y))
 PLAN = (
-    ("U", 0), ("U", 1), ("U", 2), ("R", 0), ("U", 3), ("D", 0), ("R", 1), ("U", 4), ("S1", 0), ("D", 1), ("R", 2), ("U", 5),
-    ("S2", 0), ("S1", 1), ("D", 2), ("U", 6), ("R", 3), ("F", 0), ("S2", 1), ("S1", 2), ("D", 3),
-    ("R", 4), ("U", 7), ("R", 5), ("W", 0), ("F", 1), ("S2", 2), ("D", 4), ("S1", 3), ("D", 5),
-    ("W", 1), ("F", 2), ("S1", 4), ("S2", 3), ("S1", 5), ("W", 2), ("F", 3), ("S2", 4), ("S2", 5),
-    ("W", 3), ("F", 4), ("F", 5), ("W", 4), ("W", 5),
+    ("H", 0), ("H", 1), ("H", 2), ("U", 0), ("H", 3), ("H", 4), ("H", 5), ("U", 1), ("H", 6), ("H", 7), ("U", 2),
+    ("U", 3), ("U", 4), ("U", 5), ("U", 6), ("U", 7), ("U", 8), ("R", 0), ("U", 9), ("D", 0), ("R", 1), ("R", 2),
+    ("D", 1), ("D", 2), ("S1", 0), ("S1", 1), ("S1", 2), ("S2", 0), ("S2", 1), ("S2", 2), ("F", 0), ("F", 1), ("F", 2),
+    ("W", 0), ("W", 1), ("W", 2),
 )
 
-AHEAD_FIRST = 10
+AHEAD_FIRST = 3
 AHEAD = 4
 
 GROUPED = tuple(u for u, unit in enumerate(UNITS) if unit[2] is not None)
@@ -50,8 +49,8 @@
 
 
 def mats_of(unit):
-    layer, kind, _ = unit
-    return tuple((layer, m) for m in range(3)) if kind == 0 else ((layer, 3),)
+    layer, which, _ = unit
+    return tuple((layer, m) for m in which)
 
 
 GROUPED_MATS = tuple(mat for u in GROUPED for mat in mats_of(UNITS[u]))
@@ -63,8 +62,8 @@
     w_qkv, w_out, x_in, dy_qkv, x_attn, dy_out, r_qkv, c_qkv, r_out, c_out, hyper,
     w_qkv_new, w_out_new, r_qkv_new, c_qkv_new, r_out_new, c_out_new,
     dy_part, dy_whole, x_full, x_part, g_part, g_got, g_all, wq, wo, rq, cq, ro, co,
-    pair_out, pair_in, stage, fin_out, fin_in, w_total,
-    small_sem, own_sem, dy_sem, x_send, x_recv, g_send, g_recv, pair_send, pair_recv, st_send, st_recv, fin_send, fin_recv,
+    pair_out, pair_in, stage, fin_out, fin_in, w_total, i_stat, j_stat,
+    small_sem, own_sem, dy_sem, x_send, x_recv, h_send, h_recv, g_send, g_recv, pair_send, pair_recv, st_send, st_recv, fin_send, fin_recv,
     out_sem,
 ):
     beta_two, rel_step, clip_limit = hyper[0], hyper[1], hyper[2]
@@ -72,6 +71,7 @@
     emb = lax.axis_index("emb")
     coords = tuple(lax.rem(emb // stride, RING) for stride in STRIDES)
     part = tokens // RING
+    half = part // att_size
     n_elems = float(width * width)
 
     def peer(axis, k):
@@ -110,8 +110,8 @@
     ]
 
     def x_source(u):
-        layer, kind, _ = UNITS[u]
-        return (x_in, dy_out)[kind].at[layer]
+        layer, which, _ = UNITS[u]
+        return (dy_out if which == (3,) else x_in).at[layer]
 
     def x_own(u):
         return pltpu.make_async_copy(x_source(u), x_full.at[u], own_sem.at[u])
@@ -120,8 +120,19 @@
         square = UNITS[u][2]
         device, there = mate(square, k)
         slot = GROUPED.index(u)
-        src = x_full.at[u, :, pl.ds(pl.multiple_of(there * part, part), part)]
-        return remote(src, x_part.at[slot, place_in(square)], x_send.at[slot, k - 1], x_recv.at[slot, k - 1], device)
+        src = x_full.at[u, :, pl.ds(pl.multiple_of(there * part + att * half, half), half)]
+        dst = x_part.at[slot, place_in(square), :, pl.ds(pl.multiple_of(att * half, half), half)]
+        return remote(src, dst, x_send.at[slot, k - 1], x_recv.at[slot, k - 1], device)
+
+    def hand_copy(u, k):
+        slot = GROUPED.index(u)
+        piece = x_part.at[slot, mate(UNITS[u][2], k)[1], :, pl.ds(pl.multiple_of(att * half, half), half)]
+        return remote(piece, piece, h_send.at[slot, k - 1], h_recv.at[slot, k - 1], partner)
+
+    def hand(u):
+        for k in range(1, RING):
+            x_copy(u, k).wait_recv()
+            hand_copy(u, k).start()
 
     def dy_source(mat):
         layer, m = mat
@@ -175,6 +186,8 @@
             here = place_in(UNITS[u][2])
             x_part[GROUPED.index(u), here] = x_full[u, :, pl.ds(pl.multiple_of(here * part, part), part)]
 
+    start_loads(len(loads))
+
     def g_copy(mat, k):
         device, there = mate(SQUARE_OF[mat], k)
         i = GROUPED_MATS.index(mat)
@@ -189,7 +202,7 @@
         copies = dy_copies(u)
         if u in GROUPED:
             for k in range(1, RING):
-                x_copy(u, k).wait_recv()
+                hand_copy(u, k).wait_recv()
             lhs = x_part.at[GROUPED.index(u)]
             for mat, copy in zip(mats_of(UNITS[u]), copies):
                 i = GROUPED_MATS.index(mat)
@@ -224,82 +237,89 @@
     def across(column):
         return jnp.sum(jnp.where(diag, jnp.broadcast_to(column, (16, 16)), 0.0), axis=0, keepdims=True)
 
+    def prepare():
+        for b, mats in enumerate(BATCHES):
+            tile = jnp.ones((16, 128), jnp.float32)
+            for n, (layer, m) in enumerate(mats):
+                row = co[layer : layer + 1, :] if m == 3 else rq[m, layer : layer + 1, :]
+                tile = jnp.where(lane == n, up(row), tile)
+                long = ro[layer : layer + 1, :] if m == 3 else cq[m, layer : layer + 1, :]
+                for i in range(4):
+                    j_stat[b, 4 * n + i : 4 * n + i + 1, :] = long[:, 128 * i : 128 * i + 128]
+            i_stat[b] = tile
+        w_sq = jnp.zeros((1, 128), jnp.float32)
+        for layer in range(4):
+            for m in range(4):
+                w = wo[layer] if m == 3 else wq[layer, m]
+                w_sum = jnp.sum(jnp.sum(w * w, axis=0, keepdims=True), axis=1, keepdims=True)
+                w_sq = jnp.where(lane[0:1] == layer * 4 + m, w_sum, w_sq)
+        w_total[0:1, :] = w_sq
+
     def pair_copy(b):
         return remote(pair_out.at[b], pair_in.at[b], pair_send.at[b], pair_recv.at[b], partner)
 
     def stage_copies(b, s):
-        here = coords[s]
+        here = coords[AXES[b][s]]
         out = []
         for k in range(1, RING):
-            device, _ = peer(s, k)
+            device, _ = peer(AXES[b][s], k)
             slot = stage.at[b, s, here, 0 : rows_of(b), :]
             out.append(remote(slot, slot, st_send.at[b, s, k - 1], st_recv.at[b, s, k - 1], device))
         return out
 
     def fin_copy(b):
-        return remote(fin_out.at[b], fin_in.at[b], fin_send.at[b], fin_recv.at[b], partner)
+        rows = 8 * len(BATCHES[b]) + 8
+        return remote(fin_out.at[b, 0:rows, :], fin_in.at[b, 0:rows, :], fin_send.at[b], fin_recv.at[b], partner)
 
     def step_r(b):
+        mats = BATCHES[b]
+        for mat in mats:
+            if mat in GROUPED_MATS:
+                for k in range(1, RING):
+                    g_copy(mat, k).wait_recv()
         tile = jnp.zeros((16, 128), jnp.float32)
-        for n, mat in enumerate(BATCHES[b]):
+        for n, mat in enumerate(mats):
             s = slot_of(mat)
             if mat in GROUPED_MATS:
                 i = GROUPED_MATS.index(mat)
-                total = g_part[i, place_in(SQUARE_OF[mat])]
-                for k in range(1, RING):
-                    g_copy(mat, k).wait_recv()
-                    total = total + g_got[i, k - 1]
-                g_all[s] = total
-            grad = g_all[s]
-            q_sq = grad * grad + EPS_SQUARE
-            tile = jnp.where(lane == n, jnp.sum(q_sq, axis=1, keepdims=True), tile)
+                grad = (g_part[i, place_in(SQUARE_OF[mat])] + g_got[i, 0]) + (g_got[i, 1] + g_got[i, 2])
+                g_all[s] = grad
+            else:
+                grad = g_all[s]
+            tile = jnp.where(lane == n, jnp.sum(grad * grad + EPS_SQUARE, axis=1, keepdims=True), tile)
         pair_out[b] = tile
         pair_copy(b).start()
+        out = stage.at[b, 0, coords[AXES[b][0]]]
+        for n, mat in enumerate(mats):
+            grad = g_all[slot_of(mat)]
+            q_col = jnp.sum(grad * grad + EPS_SQUARE, axis=0, keepdims=True)
+            for i in range(4):
+                out[4 * n + i : 4 * n + i + 1, :] = q_col[:, 128 * i : 128 * i + 128]
 
     def rows_of(b):
-        return 8 * len(BATCHES[b]) + (0 if b == len(BATCHES) - 1 else 8)
+        return 8 * len(BATCHES[b]) + 8
 
     def step_d(b):
-        here = coords[0]
         mats = BATCHES[b]
-        q_col = []
-        for mat in mats:
-            grad = g_all[slot_of(mat)]
-            q_col.append(jnp.sum(grad * grad + EPS_SQUARE, axis=0, keepdims=True))
-        if b == 0:
-            w_sq = jnp.zeros((1, 128), jnp.float32)
-            for layer in range(4):
-                for m in range(4):
-                    w = wo[layer] if m == 3 else wq[layer, m]
-                    w_sum = jnp.sum(jnp.sum(w * w, axis=0, keepdims=True), axis=1, keepdims=True)
-                    w_sq = jnp.where(lane[0:1] == layer * 4 + m, w_sum, w_sq)
+        count = len(mats)
         pair_copy(b).wait_recv()
-        row_total = pair_out[b] + pair_in[b]
-        out = stage.at[b, 0, here]
+        new = beta_two * i_stat[b] + (1.0 - beta_two) * ((pair_out[b] + pair_in[b]) / width)
+        i_stat[b] = new
+        root = lax.rsqrt(new)
+        out = stage.at[b, 0, coords[AXES[b][0]]]
         for n, mat in enumerate(mats):
-            layer, m = mat
             s = slot_of(mat)
-            old = co[layer : layer + 1, :] if m == 3 else rq[m, layer : layer + 1, :]
-            new = beta_two * up(old) + (1.0 - beta_two) * (row_total[:, n : n + 1] / width)
-            if m == 3:
-                co[layer : layer + 1, :] = across(new)
-            else:
-                rq[m, layer : layer + 1, :] = across(new)
-            t = g_all[s] * lax.rsqrt(new)
+            t = g_all[s] * root[:, n : n + 1]
             g_all[s] = t
             t_big = t * T_SCALE
             t_col = jnp.sum(t_big * t_big, axis=0, keepdims=True)
             for i in range(4):
-                lanes = slice(128 * i, 128 * i + 128)
-                out[8 * n + i : 8 * n + i + 1, :] = q_col[n][:, lanes]
-                out[8 * n + 4 + i : 8 * n + 5 + i, :] = t_col[:, lanes]
-            if b < len(BATCHES) - 1:
-                last = 8 * len(mats) + n
-                out[last : last + 1, :] = jnp.broadcast_to(jnp.sum(new, axis=0, keepdims=True), (1, 128))
-        if b < len(BATCHES) - 1:
-            for n in range(len(mats), 8):
-                last = 8 * len(mats) + n
-                out[last : last + 1, :] = w_sq if b == 0 and n == 4 else jnp.zeros((1, 128), jnp.float32)
+                row = 4 * (count + n) + i
+                out[row : row + 1, :] = t_col[:, 128 * i : 128 * i + 128]
+        out[8 * count : 8 * count + 8, :] = jnp.zeros((8, 128), jnp.float32)
+        out[8 * count : 8 * count + 1, :] = jnp.sum(new, axis=0, keepdims=True)
+        if b == 0:
+            out[8 * count + 1 : 8 * count + 2, :] = w_total[0:1, :]
         for copy in stage_copies(b, 0):
             copy.start()
 
@@ -310,37 +330,37 @@
         return (part_0 + part_1) + (part_2 + part_3)
 
     def step_s(b, s):
-        stage[b, s, coords[s], 0 : rows_of(b), :] = gather(b, s - 1)
+        stage[b, s, coords[AXES[b][s]], 0 : rows_of(b), :] = gather(b, s - 1)
         for copy in stage_copies(b, s):
             copy.start()
 
     def step_f(b):
+        count = len(BATCHES[b])
+        rows = 4 * count
         total = gather(b, 2)
-        mats = BATCHES[b]
-        for n, mat in enumerate(mats):
-            layer, m = mat
-            old = ro[layer : layer + 1, :] if m == 3 else cq[m, layer : layer + 1, :]
-            q_col, t_col = (
-                jnp.concatenate([total[8 * n + 4 * h + i : 8 * n + 4 * h + i + 1, :] for i in range(4)], axis=1)
-                for h in range(2)
-            )
-            new = beta_two * old + (1.0 - beta_two) * (q_col / width)
-            if m == 3:
-                ro[layer : layer + 1, :] = new
-                mean_part = jnp.sum(new, axis=1, keepdims=True)
-            else:
-                cq[m, layer : layer + 1, :] = new
-                mean_part = total[8 * len(mats) + n : 8 * len(mats) + n + 1, 0:1] * 0.5
-            v = (jnp.sqrt(t_col) * (1.0 / T_SCALE)) * lax.rsqrt(new)
-            fin_out[b, n : n + 1, :] = jnp.broadcast_to(jnp.sum(v * v, axis=1, keepdims=True), (1, 128))
-            fin_out[b, 4 + n : 5 + n, :] = jnp.broadcast_to(mean_part, (1, 128))
-        for n in range(len(mats), 4):
-            fin_out[b, n : n + 1, :] = jnp.zeros((1, 128), jnp.float32)
-            fin_out[b, 4 + n : 5 + n, :] = jnp.zeros((1, 128), jnp.float32)
-        fin_out[b, 8:16, :] = jnp.zeros((8, 128), jnp.float32)
-        if b == 0:
-            fin_out[b, 8:9, :] = total[8 * len(mats) + 4 : 8 * len(mats) + 5, :]
+        new = beta_two * j_stat[b, 0:rows, :] + (1.0 - beta_two) * (total[0:rows] / width)
+        v = (jnp.sqrt(total[rows : 2 * rows]) * (1.0 / T_SCALE)) * lax.rsqrt(new)
+        fin_out[b, 0:rows, :] = jnp.broadcast_to(jnp.sum(v * v, axis=1, keepdims=True), (rows, 128))
+        fin_out[b, rows : 2 * rows, :] = jnp.broadcast_to(jnp.sum(new, axis=1, keepdims=True), (rows, 128))
+        fin_out[b, 2 * rows : 2 * rows + 8, :] = total[2 * rows :]
         fin_copy(b).start()
+        j_stat[b, 0:rows, :] = new
+        for n, (layer, m) in enumerate(BATCHES[b]):
+            for i in range(4):
+                line = new[4 * n + i : 4 * n + i + 1, :]
+                if m == 3:
+                    ro[layer : layer + 1, 128 * i : 128 * i + 128] = line
+                else:
+                    cq[m, layer : layer + 1, 128 * i : 128 * i + 128] = line
+
+    def write_rows():
+        for b, mats in enumerate(BATCHES):
+            for n, (layer, m) in enumerate(mats):
+                line = across(i_stat[b, :, n : n + 1])
+                if m == 3:
+                    co[layer : layer + 1, :] = line
+                else:
+                    rq[m, layer : layer + 1, :] = line
 
     def out_copies(b):
         out = []
@@ -351,61 +371,78 @@
         return out
 
     def step_w(b):
+        mats = BATCHES[b]
+        rows = 4 * len(mats)
         fin_copy(b).wait_recv()
         total = fin_out[b] + fin_in[b]
         if b == 0:
-            w_total[...] = total[8:16]
-        for n, mat in enumerate(BATCHES[b]):
+            w_total[...] = total[2 * rows : 2 * rows + 8]
+
+        def four(first):
+            return (total[first : first + 1] + total[first + 1 : first + 2]) + (
+                total[first + 2 : first + 3] + total[first + 3 : first + 4]
+            )
+
+        for n, mat in enumerate(mats):
             layer, m = mat
-            mean_row = total[4 + n : 5 + n, 0:1] / width
-            rms_u = jnp.sqrt(mean_row * total[n : n + 1, 0:1] / n_elems)
-            rms_w = jnp.sqrt(w_total[0:1, slot_of(mat) : slot_of(mat) + 1] / n_elems)
+            if m == 3:
+                mean_row = four(rows + 4 * n) / width
+            else:
+                mean_row = jnp.broadcast_to(fin_out[b, 2 * rows : 2 * rows + 1, n : n + 1] / width, (1, 128))
+            rms_u = jnp.sqrt(mean_row * four(4 * n) / n_elems)
+            rms_w = jnp.sqrt(w_total[1:2, slot_of(mat) : slot_of(mat) + 1] / n_elems)
             step_size = rel_step * jnp.maximum(EPS_SCALE, rms_w) / jnp.maximum(1.0, rms_u / clip_limit)
             factor = jnp.sqrt(mean_row) * step_size
-            j_new = ro[layer : layer + 1, :] if m == 3 else cq[m, layer : layer + 1, :]
-            update = (g_all[slot_of(mat)] * lax.rsqrt(j_new)) * factor
-            if m == 3:
-                wo[layer] = wo[layer] - update
-            else:
-                wq[layer, m] = wq[layer, m] - update
+            scale = lax.rsqrt(j_stat[b, 4 * n : 4 * n + 4, :])
+            for i in range(4):
+                lanes = slice(128 * i, 128 * i + 128)
+                update = (g_all[slot_of(mat), :, lanes] * scale[i : i + 1]) * factor
+                if m == 3:
+                    wo[layer, :, lanes] = wo[layer, :, lanes] - update
+                else:
+                    wq[layer, m, :, lanes] = wq[layer, m, :, lanes] - update
         for copy in out_copies(b):
             copy.start()
 
-    waited = False
+    statistics = [
+        pltpu.make_async_copy(src, dst, out_sem.at[16 + i])
+        for i, (src, dst) in enumerate(((rq, r_qkv_new), (cq, c_qkv_new), (ro, r_out_new), (co, c_out_new)))
+    ]
+    for copy in small:
+        copy.wait()
+    prepare()
     for what, which in PLAN:
-        if what == "U":
+        if what == "H":
+            hand(which)
+        elif what == "U":
             products(which)
         elif what == "R":
             step_r(which)
         elif what == "D":
-            if not waited:
-                for copy in small:
-                    copy.wait()
-                waited = True
             step_d(which)
         elif what == "S1":
             step_s(which, 1)
         elif what == "S2":
             step_s(which, 2)
+            if which == len(BATCHES) - 1:
+                write_rows()
         elif what == "F":
             step_f(which)
         else:
+            if which == 0:
+                for copy in statistics:
+                    copy.start()
             step_w(which)
 
-    last = [
-        pltpu.make_async_copy(src, dst, out_sem.at[16 + i])
-        for i, (src, dst) in enumerate(((rq, r_qkv_new), (cq, c_qkv_new), (ro, r_out_new), (co, c_out_new)))
-    ]
-    for copy in last:
-        copy.start()
     for b in range(len(BATCHES)):
         for copy in out_copies(b):
             copy.wait()
-    for copy in last:
+    for copy in statistics:
         copy.wait()
     for u in GROUPED:
         for k in range(1, RING):
             x_copy(u, k).wait_send()
+            hand_copy(u, k).wait_send()
     for mat in GROUPED_MATS:
         for k in range(1, RING):
             g_copy(mat, k).wait_send()
@@ -465,6 +502,7 @@
         f32, bf16 = jnp.float32, jnp.bfloat16
         cols = dy_qkv.shape[3]
         n_part, n_whole, n_b = len(GROUPED_MATS), len(WHOLE), len(BATCHES)
+        most = 8 * max(len(mats) for mats in BATCHES) + 8
         dma = pltpu.SemaphoreType.DMA
         results = (w_qkv, w_out, r_qkv, c_qkv, r_out, c_out)
         out = pl.pallas_call(
@@ -488,13 +526,17 @@
                 pltpu.VMEM(c_out.shape, f32),
                 pltpu.VMEM((n_b, 16, 128), f32),
                 pltpu.VMEM((n_b, 16, 128), f32),
-                pltpu.VMEM((n_b, 3, RING, 40, 128), f32),
+                pltpu.VMEM((n_b, 3, RING, most, 128), f32),
+                pltpu.VMEM((n_b, most, 128), f32),
+                pltpu.VMEM((n_b, most, 128), f32),
+                pltpu.VMEM((8, 128), f32),
                 pltpu.VMEM((n_b, 16, 128), f32),
-                pltpu.VMEM((n_b, 16, 128), f32),
-                pltpu.VMEM((8, 128), f32),
+                pltpu.VMEM((n_b, most, 128), f32),
                 dma((6,)),
                 dma((len(UNITS),)),
                 dma((n_part + n_whole * RING,)),
+                dma((len(GROUPED), RING - 1)),
+                dma((len(GROUPED), RING - 1)),
                 dma((len(GROUPED), RING - 1)),
                 dma((len(GROUPED), RING - 1)),
                 dma((n_part, RING - 1)),

time: 59.5 us -> 47 us (0.79)
  Pallas kernels: 58.8 us -> 46.2 us
    pallas_call x1, Pallas kernels: 56.9 us -> 44.3 us  [local_run(): pl.pallas_call(functools.partial(kernel, tokens, width, att_size), out_sh...]
where the time goes in v4:
time: 47 us; the launch traced here: 46.8 us
  Pallas kernels  46.2 us (98%)
  between operations  0.64 us (1%)
    pallas_call x1, Pallas kernels, local_run(): pl.pallas_call(functools.partial(kernel, tokens, width, att_size), out_sh...  44.3 us
    pallas_call x1, Pallas kernels, local_run(): pl.pallas_call(emit, out_shape=tuple((jax.ShapeDtypeStruct(a.shape, a.dty...  1.89 us

profile of v4, /device:TPU:1, one launch (start us, length us, event | category | flops | bytes accessed | tf_op | source)
XLA Modules:
  0.0 46.8 jit_solution(9983857173189818819)
XLA Ops:
  0.6 44.3 %adafactor.1 = (f32[4,3,16,512]{3,2,1,0:T(8,128)}, f32[4,16,512]{2,1,0:T(8,128)}, f32[3,4,16]{2,1,0:T(4,128)}, f32[3,4,512]{2,1,0:T(4,128)}, f32[4,512]{1,0:T(4,128)}, /*index=5*/f32[4,16]{1,0:T(4,128)}) custom-call(f32[4,3,16,512]{3,2,1,0:T(8,128)} %w_qkv.1, f32[4,16,512]{2,1,0:T(8,128)} %bitcast.10, bf16[4,16,8192]{2,1,0:T(8,128)(2,1)} %bitcast.8, ...), custom_call_target="tpu_custom_call" | custom-call | tf_op jit(solution)/shard_map/adafactor/pallas_call | solution.py:508
  44.9 1.9 %emit.1 = (f32[4,3,16,512]{3,2,1,0:T(8,128)}, f32[4,16,512]{2,1,0:T(8,128)}, f32[3,4,16]{2,1,0:T(4,128)}, f32[3,4,512]{2,1,0:T(4,128)}, f32[4,512]{1,0:T(4,128)}, /*index=5*/f32[4,16]{1,0:T(4,128)}) custom-call(f32[4,3,16,512]{3,2,1,0:T(8,128)} %get-tuple-element.18.refs_0_, f32[4,16,512]{2,1,0:T(8,128)} %get-tuple-element.19.refs_1_, ...), custom_call_target="tpu_custom_call" | custom-call | tf_op jit(solution)/shard_map/emit/pallas_call | solution.py:557

commit v5 on v4

--- a/solution.py
+++ b/solution.py
@@ -17,32 +17,27 @@
 
 SQUARES = (((X, 0), (Y, 0)), ((Y, 1), (Z, 0)), ((Z, 1), (X, 1)))
 UNITS = (
-    (0, (0, 1, 2), 0),
-    (1, (0, 1, 2), 1),
-    (2, (0, 1, 2), 2),
-    (3, (0,), 0),
-    (3, (1,), 1),
-    (3, (2,), 2),
-    (0, (3,), 0),
-    (1, (3,), 1),
-    (2, (3,), None),
-    (3, (3,), None),
+    tuple((layer, (0, 1, 2), layer) for layer in range(3))
+    + tuple((3, (m,), m) for m in range(3))
+    + tuple((layer, (3,), None) for layer in range(4))
 )
-BATCHES = (
-    ((0, 0), (0, 1), (0, 2), (1, 0), (1, 1), (1, 2)),
-    ((2, 0), (2, 1), (2, 2), (3, 0), (2, 3), (3, 3)),
-    ((3, 1), (3, 2), (0, 3), (1, 3)),
+PRODUCTS = (
+    (((0, 3),),)
+    + tuple(tuple((layer, m) for layer in range(3)) for m in range(3))
+    + (tuple((3, m) for m in range(3)),)
+    + tuple(((layer, 3),) for layer in range(1, 4))
 )
-AXES = ((X, Y, Z), (Y, Z, X), (Z, X, Y))
+READY = PRODUCTS[1] + PRODUCTS[0] + sum(PRODUCTS[2:], ())
+BATCHES = tuple(READY[first : first + 4] for first in range(0, len(READY), 4))
+CUBES = tuple(tuple((axis, first) for axis in (X, Y, Z)) for first in range(2))
+ORDERS = tuple((b % 2, 1 - b % 2) for b in range(len(BATCHES)))
+CUBE = 8
 PLAN = (
-    ("H", 0), ("H", 1), ("H", 2), ("U", 0), ("H", 3), ("H", 4), ("H", 5), ("U", 1), ("H", 6), ("H", 7), ("U", 2),
-    ("U", 3), ("U", 4), ("U", 5), ("U", 6), ("U", 7), ("U", 8), ("R", 0), ("U", 9), ("D", 0), ("R", 1), ("R", 2),
-    ("D", 1), ("D", 2), ("S1", 0), ("S1", 1), ("S1", 2), ("S2", 0), ("S2", 1), ("S2", 2), ("F", 0), ("F", 1), ("F", 2),
-    ("W", 0), ("W", 1), ("W", 2),
+    "U0", "H0", "H1", "H2", "U1", "H3", "H4", "H5", "U2", "U3", "U4", "R0", "U5", "D0", "R1", "U6", "D1", "R2", "U7", "D2",
+    "R3", "A0", "D3", "A1", "A2", "F0", "A3", "W0", "F1", "W1", "F2", "W2", "F3", "W3",
 )
-
-AHEAD_FIRST = 3
-AHEAD = 4
+AHEAD = 3
+SLOTS = 26
 
 GROUPED = tuple(u for u, unit in enumerate(UNITS) if unit[2] is not None)
 WHOLE = tuple(u for u, unit in enumerate(UNITS) if unit[2] is None)
@@ -54,6 +49,10 @@
 
 
 GROUPED_MATS = tuple(mat for u in GROUPED for mat in mats_of(UNITS[u]))
+UNIT_OF = {mat: u for u, unit in enumerate(UNITS) for mat in mats_of(unit)}
+BLOCKS = tuple(
+    (mat, j) for mats in PRODUCTS for mat in mats for j in ((None,) if mat in GROUPED_MATS else range(RING))
+)
 SQUARE_OF = {mat: UNITS[u][2] for u in GROUPED for mat in mats_of(UNITS[u])}
 
 
@@ -61,7 +60,7 @@
     tokens, width, att_size,
     w_qkv, w_out, x_in, dy_qkv, x_attn, dy_out, r_qkv, c_qkv, r_out, c_out, hyper,
     w_qkv_new, w_out_new, r_qkv_new, c_qkv_new, r_out_new, c_out_new,
-    dy_part, dy_whole, x_full, x_part, g_part, g_got, g_all, wq, wo, rq, cq, ro, co,
+    dy, x_full, x_part, g_part, g_got, g_all, wq, wo, rq, cq, ro, co,
     pair_out, pair_in, stage, fin_out, fin_in, w_total, i_stat, j_stat,
     small_sem, own_sem, dy_sem, x_send, x_recv, h_send, h_recv, g_send, g_recv, pair_send, pair_recv, st_send, st_recv, fin_send, fin_recv,
     out_sem,
@@ -74,20 +73,15 @@
     half = part // att_size
     n_elems = float(width * width)
 
-    def peer(axis, k):
-        place = lax.rem(coords[axis] + k, RING)
-        return (att, emb + (place - coords[axis]) * STRIDES[axis]), place
-
     def bit(axis, first):
         return lax.rem(coords[axis] + first, 2)
 
-    def place_in(square):
-        (axis_a, first_a), (axis_b, first_b) = SQUARES[square]
-        return bit(axis_a, first_a) + 2 * bit(axis_b, first_b)
-
-    def mate(square, k):
-        index, place = emb, place_in(square)
-        for n, (axis, first) in enumerate(SQUARES[square]):
+    def place_in(pairs):
+        return sum(bit(axis, first) * (1 << n) for n, (axis, first) in enumerate(pairs))
+
+    def mate(pairs, k):
+        index, place = emb, place_in(pairs)
+        for n, (axis, first) in enumerate(pairs):
             if k & (1 << n):
                 here = bit(axis, first)
                 there = lax.rem(coords[axis] + RING + 1 - 2 * here, RING)
@@ -118,15 +112,15 @@
 
     def x_copy(u, k):
         square = UNITS[u][2]
-        device, there = mate(square, k)
+        device, there = mate(SQUARES[square], k)
         slot = GROUPED.index(u)
         src = x_full.at[u, :, pl.ds(pl.multiple_of(there * part + att * half, half), half)]
-        dst = x_part.at[slot, place_in(square), :, pl.ds(pl.multiple_of(att * half, half), half)]
+        dst = x_part.at[slot, place_in(SQUARES[square]), :, pl.ds(pl.multiple_of(att * half, half), half)]
         return remote(src, dst, x_send.at[slot, k - 1], x_recv.at[slot, k - 1], device)
 
     def hand_copy(u, k):
         slot = GROUPED.index(u)
-        piece = x_part.at[slot, mate(UNITS[u][2], k)[1], :, pl.ds(pl.multiple_of(att * half, half), half)]
+        piece = x_part.at[slot, mate(SQUARES[UNITS[u][2]], k)[1], :, pl.ds(pl.multiple_of(att * half, half), half)]
         return remote(piece, piece, h_send.at[slot, k - 1], h_recv.at[slot, k - 1], partner)
 
     def hand(u):
@@ -138,42 +132,27 @@
         layer, m = mat
         return dy_qkv.at[layer, m] if m < 3 else x_attn.at[layer]
 
-    def dy_copies(u):
-        out = []
-        for mat in mats_of(UNITS[u]):
-            if u in GROUPED:
-                i = GROUPED_MATS.index(mat)
-                here = place_in(UNITS[u][2])
-                src = dy_source(mat).at[pl.ds(pl.multiple_of(here * part, part), part), :]
-                out.append(pltpu.make_async_copy(src, dy_part.at[i], dy_sem.at[i]))
-            else:
-                for j in range(RING):
-                    w = WHOLE.index(u)
-                    rows = pl.ds(j * part, part)
-                    out.append(
-                        pltpu.make_async_copy(
-                            dy_source(mat).at[rows, :], dy_whole.at[w, rows, :], dy_sem.at[len(GROUPED_MATS) + w * RING + j]
-                        )
-                    )
-        return out
+    def dy_copy(c):
+        mat, j = BLOCKS[c]
+        start = j * part if j is not None else pl.multiple_of(place_in(SQUARES[SQUARE_OF[mat]]) * part, part)
+        return pltpu.make_async_copy(dy_source(mat).at[pl.ds(start, part), :], dy.at[c % SLOTS], dy_sem.at[c])
 
     for u in range(len(UNITS)):
         x_own(u).start()
     for copy in small:
         copy.start()
-    loads = [copy for u in range(len(UNITS)) for copy in dy_copies(u)]
-    started = [0]
+    started, used = [0], [0]
 
     def start_loads(upto):
-        for copy in loads[started[0] : upto]:
-            copy.start()
-        started[0] = max(started[0], min(upto, len(loads)))
-
-    start_loads(AHEAD_FIRST)
+        for c in range(started[0], upto):
+            dy_copy(c).start()
+        started[0] = max(started[0], upto)
+
+    start_loads(AHEAD)
 
     barrier = pltpu.get_barrier_semaphore()
-    neighbours = [peer(axis, k)[0] for axis in (X, Y, Z) for k in range(1, RING)] + [partner]
-    neighbours += [mate(square, 3)[0] for square in range(len(SQUARES))]
+    neighbours = [mate(cube, k)[0] for cube in CUBES for k in range(1, CUBE)] + [partner]
+    neighbours += [mate(SQUARES[square], 3)[0] for square in range(1, len(SQUARES))]
     for device in neighbours:
         pl.semaphore_signal(barrier, inc=1, device_id=device, device_id_type=pl.DeviceIdType.MESH)
     pl.semaphore_wait(barrier, len(neighbours))
@@ -183,50 +162,51 @@
         if u in GROUPED:
             for k in (3, 1, 2):
                 x_copy(u, k).start()
-            here = place_in(UNITS[u][2])
+            here = place_in(SQUARES[UNITS[u][2]])
             x_part[GROUPED.index(u), here] = x_full[u, :, pl.ds(pl.multiple_of(here * part, part), part)]
 
-    start_loads(len(loads))
+    start_loads(SLOTS)
 
     def g_copy(mat, k):
-        device, there = mate(SQUARE_OF[mat], k)
+        device, there = mate(SQUARES[SQUARE_OF[mat]], k)
         i = GROUPED_MATS.index(mat)
         return remote(g_part.at[i, there], g_got.at[i, k - 1], g_send.at[i, k - 1], g_recv.at[i, k - 1], device)
 
     def slot_of(mat):
         return mat[0] * 4 + mat[1]
 
-    done = [0]
-
-    def products(u):
-        copies = dy_copies(u)
+    handed = set()
+
+    def products(mats):
+        u = UNIT_OF[mats[0]]
+        first = used[0]
         if u in GROUPED:
-            for k in range(1, RING):
-                hand_copy(u, k).wait_recv()
-            lhs = x_part.at[GROUPED.index(u)]
-            for mat, copy in zip(mats_of(UNITS[u]), copies):
+            for n, mat in enumerate(mats):
+                u = UNIT_OF[mat]
+                if u not in handed:
+                    handed.add(u)
+                    for k in range(1, RING):
+                        hand_copy(u, k).wait_recv()
+                dy_copy(first + n).wait()
+            for n, mat in enumerate(mats):
                 i = GROUPED_MATS.index(mat)
-                copy.wait()
-                done[0] += 1
-                start_loads(done[0] + AHEAD)
-                got = jnp.dot(
-                    lhs[...].reshape(RING * 16, part), dy_part[i], preferred_element_type=jnp.float32
-                )
+                lhs = x_part[GROUPED.index(UNIT_OF[mat])].reshape(RING * 16, part)
+                got = jnp.dot(lhs, dy[(first + n) % SLOTS], preferred_element_type=jnp.float32)
                 g_part[i] = got.reshape(RING, 16, got.shape[1])
-                for k in range(1, RING):
+            for mat in mats:
+                for k in (3, 1, 2):
                     g_copy(mat, k).start()
+            used[0] += len(mats)
         else:
-            w = WHOLE.index(u)
-            (mat,) = mats_of(UNITS[u])
             total = None
-            for j, copy in enumerate(copies):
-                copy.wait()
-                done[0] += 1
-                start_loads(done[0] + AHEAD)
+            for j in range(RING):
+                dy_copy(first + j).wait()
                 rows = pl.ds(j * part, part)
-                got = jnp.dot(x_full[u, :, rows], dy_whole[w, rows, :], preferred_element_type=jnp.float32)
+                got = jnp.dot(x_full[u, :, rows], dy[(first + j) % SLOTS], preferred_element_type=jnp.float32)
                 total = got if total is None else total + got
-            g_all[slot_of(mat)] = total
+            g_all[slot_of(mats[0])] = total
+            used[0] += RING
+        start_loads(min(len(BLOCKS), SLOTS + used[0]))
 
     diag = lax.broadcasted_iota(jnp.int32, (16, 16), 0) == lax.broadcasted_iota(jnp.int32, (16, 16), 1)
     lane = lax.broadcasted_iota(jnp.int32, (16, 128), 1)
@@ -259,10 +239,10 @@
         return remote(pair_out.at[b], pair_in.at[b], pair_send.at[b], pair_recv.at[b], partner)
 
     def stage_copies(b, s):
-        here = coords[AXES[b][s]]
+        here = place_in(CUBES[ORDERS[b][s]])
         out = []
-        for k in range(1, RING):
-            device, _ = peer(AXES[b][s], k)
+        for k in (7, 6, 5, 3, 4, 2, 1):
+            device, _ = mate(CUBES[ORDERS[b][s]], k)
             slot = stage.at[b, s, here, 0 : rows_of(b), :]
             out.append(remote(slot, slot, st_send.at[b, s, k - 1], st_recv.at[b, s, k - 1], device))
         return out
@@ -282,14 +262,14 @@
             s = slot_of(mat)
             if mat in GROUPED_MATS:
                 i = GROUPED_MATS.index(mat)
-                grad = (g_part[i, place_in(SQUARE_OF[mat])] + g_got[i, 0]) + (g_got[i, 1] + g_got[i, 2])
+                grad = (g_part[i, place_in(SQUARES[SQUARE_OF[mat]])] + g_got[i, 0]) + (g_got[i, 1] + g_got[i, 2])
                 g_all[s] = grad
             else:
                 grad = g_all[s]
             tile = jnp.where(lane == n, jnp.sum(grad * grad + EPS_SQUARE, axis=1, keepdims=True), tile)
         pair_out[b] = tile
         pair_copy(b).start()
-        out = stage.at[b, 0, coords[AXES[b][0]]]
+        out = stage.at[b, 0, place_in(CUBES[ORDERS[b][0]])]
         for n, mat in enumerate(mats):
             grad = g_all[slot_of(mat)]
             q_col = jnp.sum(grad * grad + EPS_SQUARE, axis=0, keepdims=True)
@@ -306,7 +286,7 @@
         new = beta_two * i_stat[b] + (1.0 - beta_two) * ((pair_out[b] + pair_in[b]) / width)
         i_stat[b] = new
         root = lax.rsqrt(new)
-        out = stage.at[b, 0, coords[AXES[b][0]]]
+        out = stage.at[b, 0, place_in(CUBES[ORDERS[b][0]])]
         for n, mat in enumerate(mats):
             s = slot_of(mat)
             t = g_all[s] * root[:, n : n + 1]
@@ -326,18 +306,20 @@
     def gather(b, s):
         for copy in stage_copies(b, s):
             copy.wait_recv()
-        part_0, part_1, part_2, part_3 = (stage[b, s, i, 0 : rows_of(b), :] for i in range(RING))
-        return (part_0 + part_1) + (part_2 + part_3)
+        parts = [stage[b, s, i, 0 : rows_of(b), :] for i in range(CUBE)]
+        while len(parts) > 1:
+            parts = [parts[i] + parts[i + 1] for i in range(0, len(parts), 2)]
+        return parts[0]
 
     def step_s(b, s):
-        stage[b, s, coords[AXES[b][s]], 0 : rows_of(b), :] = gather(b, s - 1)
+        stage[b, s, place_in(CUBES[ORDERS[b][s]]), 0 : rows_of(b), :] = gather(b, s - 1)
         for copy in stage_copies(b, s):
             copy.start()
 
     def step_f(b):
         count = len(BATCHES[b])
         rows = 4 * count
-        total = gather(b, 2)
+        total = gather(b, 1)
         new = beta_two * j_stat[b, 0:rows, :] + (1.0 - beta_two) * (total[0:rows] / width)
         v = (jnp.sqrt(total[rows : 2 * rows]) * (1.0 / T_SCALE)) * lax.rsqrt(new)
         fin_out[b, 0:rows, :] = jnp.broadcast_to(jnp.sum(v * v, axis=1, keepdims=True), (rows, 128))
@@ -411,27 +393,26 @@
     for copy in small:
         copy.wait()
     prepare()
-    for what, which in PLAN:
+    for step in PLAN:
+        what, which = step[0], int(step[1])
         if what == "H":
             hand(which)
         elif what == "U":
-            products(which)
+            products(PRODUCTS[which])
         elif what == "R":
             step_r(which)
         elif what == "D":
             step_d(which)
-        elif what == "S1":
+        elif what == "A":
             step_s(which, 1)
-        elif what == "S2":
-            step_s(which, 2)
             if which == len(BATCHES) - 1:
                 write_rows()
         elif what == "F":
             step_f(which)
-        else:
-            if which == 0:
+            if which == len(BATCHES) - 1:
                 for copy in statistics:
                     copy.start()
+        else:
             step_w(which)
 
     for b in range(len(BATCHES)):
@@ -449,7 +430,7 @@
     for b in range(len(BATCHES)):
         pair_copy(b).wait_send()
         fin_copy(b).wait_send()
-        for s in range(3):
+        for s in range(2):
             for copy in stage_copies(b, s):
                 copy.wait_send()
 
@@ -501,7 +482,7 @@
         c_qkv = jnp.swapaxes(c_qkv, 0, 1)
         f32, bf16 = jnp.float32, jnp.bfloat16
         cols = dy_qkv.shape[3]
-        n_part, n_whole, n_b = len(GROUPED_MATS), len(WHOLE), len(BATCHES)
+        n_part, n_b = len(GROUPED_MATS), len(BATCHES)
         most = 8 * max(len(mats) for mats in BATCHES) + 8
         dma = pltpu.SemaphoreType.DMA
         results = (w_qkv, w_out, r_qkv, c_qkv, r_out, c_out)
@@ -511,8 +492,7 @@
             in_specs=[pl.BlockSpec(memory_space=pl.ANY)] * 10 + [pl.BlockSpec(memory_space=pltpu.SMEM)],
             out_specs=tuple(pl.BlockSpec(memory_space=pl.ANY) for _ in results),
             scratch_shapes=[
-                pltpu.VMEM((n_part, part, cols), bf16),
-                pltpu.VMEM((n_whole, tokens, cols), bf16),
+                pltpu.VMEM((SLOTS, part, cols), bf16),
                 pltpu.VMEM((len(UNITS), 16, tokens), bf16),
                 pltpu.VMEM((len(GROUPED), RING, 16, part), bf16),
                 pltpu.VMEM((n_part, RING, 16, cols), f32),
@@ -526,7 +506,7 @@
                 pltpu.VMEM(c_out.shape, f32),
                 pltpu.VMEM((n_b, 16, 128), f32),
                 pltpu.VMEM((n_b, 16, 128), f32),
-                pltpu.VMEM((n_b, 3, RING, most, 128), f32),
+                pltpu.VMEM((n_b, 2, CUBE, most, 128), f32),
                 pltpu.VMEM((n_b, most, 128), f32),
                 pltpu.VMEM((n_b, most, 128), f32),
                 pltpu.VMEM((8, 128), f32),
@@ -534,7 +514,7 @@
                 pltpu.VMEM((n_b, most, 128), f32),
                 dma((6,)),
                 dma((len(UNITS),)),
-                dma((n_part + n_whole * RING,)),
+                dma((len(BLOCKS),)),
                 dma((len(GROUPED), RING - 1)),
                 dma((len(GROUPED), RING - 1)),
                 dma((len(GROUPED), RING - 1)),
@@ -543,8 +523,8 @@
                 dma((n_part, RING - 1)),
                 dma((n_b,)),
                 dma((n_b,)),
-                dma((n_b, 3, RING - 1)),
-                dma((n_b, 3, RING - 1)),
+                dma((n_b, 2, CUBE - 1)),
+                dma((n_b, 2, CUBE - 1)),
                 dma((n_b,)),
                 dma((n_b,)),
                 dma((20,)),

time: 47 us -> 44.9 us (0.955)
  Pallas kernels: 46.2 us -> 44.1 us
    pallas_call x1, Pallas kernels: 44.3 us -> 42.2 us  [local_run(): pl.pallas_call(functools.partial(kernel, tokens, width, att_size), out_sh...]
where the time goes in v5:
time: 44.9 us; the launch traced here: 44.7 us
  Pallas kernels  44.1 us (98%)
  between operations  0.64 us (1%)
    pallas_call x1, Pallas kernels, local_run(): pl.pallas_call(functools.partial(kernel, tokens, width, att_size), out_sh...  42.2 us
    pallas_call x1, Pallas kernels, local_run(): pl.pallas_call(emit, out_shape=tuple((jax.ShapeDtypeStruct(a.shape, a.dty...  1.89 us

profile of v5, /device:TPU:1, one launch (start us, length us, event | category | flops | bytes accessed | tf_op | source)
XLA Modules:
  0.0 44.7 jit_solution(5505292263790548079)
XLA Ops:
  0.6 42.2 %adafactor.1 = (f32[4,3,16,512]{3,2,1,0:T(8,128)}, f32[4,16,512]{2,1,0:T(8,128)}, f32[3,4,16]{2,1,0:T(4,128)}, f32[3,4,512]{2,1,0:T(4,128)}, f32[4,512]{1,0:T(4,128)}, /*index=5*/f32[4,16]{1,0:T(4,128)}) custom-call(f32[4,3,16,512]{3,2,1,0:T(8,128)} %w_qkv.1, f32[4,16,512]{2,1,0:T(8,128)} %bitcast.10, bf16[4,16,8192]{2,1,0:T(8,128)(2,1)} %bitcast.8, ...), custom_call_target="tpu_custom_call" | custom-call | tf_op jit(solution)/shard_map/adafactor/pallas_call | solution.py:489
  42.8 1.9 %emit.1 = (f32[4,3,16,512]{3,2,1,0:T(8,128)}, f32[4,16,512]{2,1,0:T(8,128)}, f32[3,4,16]{2,1,0:T(4,128)}, f32[3,4,512]{2,1,0:T(4,128)}, f32[4,512]{1,0:T(4,128)}, /*index=5*/f32[4,16]{1,0:T(4,128)}) custom-call(f32[4,3,16,512]{3,2,1,0:T(8,128)} %get-tuple-element.18.refs_0_, f32[4,16,512]{2,1,0:T(8,128)} %get-tuple-element.19.refs_1_, ...), custom_call_target="tpu_custom_call" | custom-call | tf_op jit(solution)/shard_map/emit/pallas_call | solution.py:537

commit v6 on v5

--- a/solution.py
+++ b/solution.py
@@ -33,8 +33,8 @@
 ORDERS = tuple((b % 2, 1 - b % 2) for b in range(len(BATCHES)))
 CUBE = 8
 PLAN = (
-    "U0", "H0", "H1", "H2", "U1", "H3", "H4", "H5", "U2", "U3", "U4", "R0", "U5", "D0", "R1", "U6", "D1", "R2", "U7", "D2",
-    "R3", "A0", "D3", "A1", "A2", "F0", "A3", "W0", "F1", "W1", "F2", "W2", "F3", "W3",
+    "U0", "H0", "H1", "H2", "U1", "H3", "H4", "H5", "U2", "U3", "U4", "R0", "U5", "D0", "R1", "U6", "D1", "U7", "R2", "R3",
+    "D2", "A0", "D3", "A1", "A2", "F0", "A3", "W0", "F1", "W1", "F2", "W2", "F3", "W3",
 )
 AHEAD = 3
 SLOTS = 26

time: 44.9 us -> 45.6 us (1.016)
  Pallas kernels: 44.1 us -> 44.8 us
    pallas_call x1, Pallas kernels: 42.2 us -> 42.9 us  [local_run(): pl.pallas_call(functools.partial(kernel, tokens, width, att_size), out_sh...]
where the time goes in v6:
time: 45.6 us; the launch traced here: 45.5 us
  Pallas kernels  44.8 us (98%)
  between operations  0.64 us (1%)
    pallas_call x1, Pallas kernels, local_run(): pl.pallas_call(functools.partial(kernel, tokens, width, att_size), out_sh...  42.9 us
    pallas_call x1, Pallas kernels, local_run(): pl.pallas_call(emit, out_shape=tuple((jax.ShapeDtypeStruct(a.shape, a.dty...  1.89 us

profile of v6, /device:TPU:1, one launch (start us, length us, event | category | flops | bytes accessed | tf_op | source)
XLA Modules:
  0.0 45.5 jit_solution(302107736277545238)
XLA Ops:
  0.6 42.9 %adafactor.1 = (f32[4,3,16,512]{3,2,1,0:T(8,128)}, f32[4,16,512]{2,1,0:T(8,128)}, f32[3,4,16]{2,1,0:T(4,128)}, f32[3,4,512]{2,1,0:T(4,128)}, f32[4,512]{1,0:T(4,128)}, /*index=5*/f32[4,16]{1,0:T(4,128)}) custom-call(f32[4,3,16,512]{3,2,1,0:T(8,128)} %w_qkv.1, f32[4,16,512]{2,1,0:T(8,128)} %bitcast.10, bf16[4,16,8192]{2,1,0:T(8,128)(2,1)} %bitcast.8, ...), custom_call_target="tpu_custom_call" | custom-call | tf_op jit(solution)/shard_map/adafactor/pallas_call | solution.py:489
  43.6 1.9 %emit.1 = (f32[4,3,16,512]{3,2,1,0:T(8,128)}, f32[4,16,512]{2,1,0:T(8,128)}, f32[3,4,16]{2,1,0:T(4,128)}, f32[3,4,512]{2,1,0:T(4,128)}, f32[4,512]{1,0:T(4,128)}, /*index=5*/f32[4,16]{1,0:T(4,128)}) custom-call(f32[4,3,16,512]{3,2,1,0:T(8,128)} %get-tuple-element.18.refs_0_, f32[4,16,512]{2,1,0:T(8,128)} %get-tuple-element.19.refs_1_, ...), custom_call_target="tpu_custom_call" | custom-call | tf_op jit(solution)/shard_map/emit/pallas_call | solution.py:537
